TPU v7x, 32 devices: a whole 2x2x4 slice. The times are simulated.
32 devices in a mesh: dp: 8 (over z, y), seq: 4 (over x, core).
Axes of the slice: x: 2, y: 2, z: 4, core: 2. Of those that a mesh axis runs over, the one named last changes fastest.
Arguments:
- tokens: bfloat16 [16, 1024, 1536], P('dp', 'seq'), may hold values from -6 to 6
- in_proj: bfloat16 [1536, 6448], P(('dp', 'seq')), may hold values from -0.15625 to 0.15625
- conv_weight: bfloat16 [4, 3328], P(None, ('dp', 'seq')), may hold values from -3 to 3
- conv_bias: bfloat16 [3328], P(('dp', 'seq')), may hold values from -0.5 to 0.5
- decay_log: float32 [48], replicated, may hold values from -6 to 0.5
- step_bias: float32 [48], replicated, may hold values from -4.5 to -2
- skip_gain: float32 [48], replicated, may hold values from 0.5 to 1.5
- norm_gain: bfloat16 [1536], P(('dp', 'seq')), may hold values from 0.099609375 to 1.8984375
- gated_gain: bfloat16 [3072], P(('dp', 'seq')), may hold values from 0.099609375 to 1.8984375
- out_proj: bfloat16 [3072, 1536], P(('dp', 'seq')), may hold values from -0.109375 to 0.109375
- cotangent: bfloat16 [16, 1024, 1536], P('dp', 'seq'), may hold values from -6 to 6
Outputs:
- block_out: bfloat16 [16, 1024, 1536], P('dp', 'seq')
- tokens_grad: bfloat16 [16, 1024, 1536], P('dp', 'seq')
- in_proj_grad: float32 [1536, 6448], P(('dp', 'seq'))
- conv_weight_grad: float32 [4, 3328], P(None, ('dp', 'seq'))
- conv_bias_grad: float32 [3328], P(('dp', 'seq'))
- decay_log_grad: float32 [48], replicated
- step_bias_grad: float32 [48], replicated
- skip_gain_grad: float32 [48], replicated
- norm_gain_grad: float32 [1536], P(('dp', 'seq'))
- gated_gain_grad: float32 [3072], P(('dp', 'seq'))
- out_proj_grad: float32 [3072, 1536], P(('dp', 'seq'))
All inputs are finite; a program needn't handle non-finite values.
Results may differ from a plain program's by a relative error of at most 0.0062.
Values may be sent and summed in bfloat16 or wider, within the bound.
A program may use at most 256 MiB of HBM per device.

v0:
```python
import functools

import jax
import jax.numpy as jnp
from jax import lax
from jax.experimental import pallas as pl
from jax.experimental.pallas import tpu as pltpu
from jax.sharding import PartitionSpec as P

HEADS = 48
P_SIZE = 64
N = 128
KW = 4
DI = 3072
CD = 3328
LANES = 128
FAR = -1e30

EPSILON = 1e-05
F32 = jnp.float32
BF16 = jnp.bfloat16


def dot(a, b, dims=((1,), (0,)), precision=None):
    return lax.dot_general(a, b, (dims, ((), ())), precision=precision, preferred_element_type=F32)


NT = ((1,), (1,))
HIGH = lax.Precision.HIGHEST


def pick(a, p, low):
    return jnp.where(low, a[:, 2 * p : 2 * p + 1], a[:, 2 * p + 1 : 2 * p + 2])


def chunk_parts(heads, rest_ref, xbuf, taps_ref, head_ref):
    size = rest_ref.shape[0]
    wide = taps_ref.shape[1]
    mixed = taps_ref[KW : KW + 1, :] + taps_ref[0:1, :] * xbuf[5 : 5 + size, :]
    for k in range(1, KW):
        mixed = mixed + taps_ref[k : k + 1, :] * xbuf[5 + k : 5 + k + size, :]
    sig = lax.logistic(mixed)
    lane = lax.broadcasted_iota(jnp.int32, (1, LANES), 1)
    raw = jnp.where(lane < heads, rest_ref[:, wide:], 0.0) + head_ref[1:2, :]
    step = jnp.maximum(raw, 0.0) + jnp.log1p(jnp.exp(-jnp.abs(raw)))
    decay = -jnp.exp(head_ref[0:1, :]) * step
    i = lax.broadcasted_iota(jnp.int32, (size, size), 0)
    j = lax.broadcasted_iota(jnp.int32, (size, size), 1)
    run = dot(jnp.where(i >= j, 1.0, 0.0), decay, precision=HIGH)
    return mixed, sig, raw, step, decay, run


def backward_kernel(
    heads,
    rest_ref,
    prev_ref,
    dy_ref,
    mem_ref,
    taps_ref,
    head_ref,
    out_ref,
    wgrad_ref,
    hgrad_ref,
    xbuf,
    gbuf,
    adj,
    dmix,
    dsum,
    uprod,
    zprod,
    rows_t,
    line,
):
    size = rest_ref.shape[0]
    wide = taps_ref.shape[1]
    inner = heads * P_SIZE
    chunks = pl.num_programs(1)
    step_id = pl.program_id(1)
    newest = step_id == 0
    oldest = step_id == chunks - 1
    begin = jnp.logical_and(pl.program_id(0) == 0, newest)
    finish = jnp.logical_and(pl.program_id(0) == pl.num_programs(0) - 1, oldest)

    @pl.when(begin)
    def _():
        wgrad_ref[...] = jnp.zeros_like(wgrad_ref)
        hgrad_ref[...] = jnp.zeros_like(hgrad_ref)
        rows_t[...] = jnp.zeros_like(rows_t)
        line[...] = jnp.zeros_like(line)

    @pl.when(newest)
    def _():
        gbuf[size : size + 8, :] = jnp.zeros((8, wide), F32)
        adj[...] = jnp.zeros_like(adj)

    @pl.when(jnp.logical_not(newest))
    def _():
        gbuf[size : size + 8, :] = gbuf[0:8, :]

    xbuf[0:8, :] = jnp.where(oldest, 0.0, prev_ref[:, :wide])
    xbuf[8 : 8 + size, :] = rest_ref[:, :wide]
    mixed, sig, raw, step, decay, run = chunk_parts(heads, rest_ref, xbuf, taps_ref, head_ref)
    act = mixed * sig
    run_t = run.T
    closing = run[size - 1 : size, :]
    last = jnp.exp(closing)
    left = jnp.exp(closing - run)
    grown = jnp.exp(run)
    b = act[:, inner : inner + N].astype(BF16)
    c = act[:, inner + N :].astype(BF16)
    c_t = act[:, inner + N :].T.astype(BF16)
    scores_t = dot(b, c, NT)
    low = lax.broadcasted_iota(jnp.int32, (1, LANES), 1) < P_SIZE
    lane = lax.broadcasted_iota(jnp.int32, (1, LANES), 1)
    j = lax.broadcasted_iota(jnp.int32, (size, size), 0)
    i = lax.broadcasted_iota(jnp.int32, (size, size), 1)
    causal = i >= j
    mem_b = mem_ref[0]
    adj_b = adj[...].astype(BF16)
    spread = dot(b, adj_b)
    inherit = dot(c, mem_b)
    scored = jnp.zeros((size, size), F32)
    cols = jnp.zeros((size, LANES), F32)
    for p in range(heads // 2):
        at = slice(p * LANES, (p + 1) * LANES)
        v = act[:, at]
        size_p = pick(step, p, low)
        xv = size_p * v
        dy = dy_ref[:, at]
        dyb = dy.astype(BF16)
        xvb = xv.astype(BF16)
        dxv = pick(left, p, low) * spread[:, at]
        zprod[:, at] = (dxv * xv).astype(BF16)
        dyg = pick(grown, p, low) * dy
        uprod[:, at] = (dyg * inherit[:, at]).astype(BF16)
        for e in range(2):
            h = 2 * p + e
            keep = low if e == 0 else jnp.logical_not(low)
            mine = jnp.where(keep, dy, 0.0).astype(BF16)
            gap = run_t[h : h + 1, :] - run[:, h : h + 1]
            near = jnp.exp(jnp.where(causal, gap, FAR))
            w_t = scores_t * near
            dw_t = dot(xvb, mine, NT)
            scored = scored + dw_t * near
            g_t = dw_t * w_t
            rows_t[h : h + 1, :] = jnp.sum(g_t, axis=0, keepdims=True)
            cols = jnp.where(lane == h, jnp.sum(g_t, axis=1, keepdims=True), cols)
            dxv = dxv + dot(w_t.astype(BF16), mine)
        dsum[:, at] = (dxv * v).astype(BF16)
        dmix[:, at] = size_p * dxv + pick(head_ref[2:3, :], p, low) * dy
        line[0:1, at] += jnp.sum(dy * v, axis=0, keepdims=True)
        line[1:2, at] = jnp.sum(adj[:, at] * mem_b[:, at].astype(F32), axis=0, keepdims=True) * pick(
            last, p, low
        )
        xc = (pick(left, p, low) * xv).astype(BF16)
        dygb = dyg.astype(BF16)
        db = dot(xc, adj_b[:, at], NT)
        dc = dot(dygb, mem_b[:, at], NT)
        if p == 0:
            dmix[:, inner : inner + N] = db
            dmix[:, inner + N :] = dc
        else:
            dmix[:, inner : inner + N] += db
            dmix[:, inner + N :] += dc
        adj[:, at] = adj[:, at] * pick(last, p, low) + dot(c_t, dygb)
    dmix[:, inner : inner + N] += dot(scored.astype(BF16), c)
    dmix[:, inner + N :] += dot(scored.T.astype(BF16), b)

    group = jnp.where(
        lax.broadcasted_iota(jnp.int32, (inner, LANES), 0) // P_SIZE
        == lax.broadcasted_iota(jnp.int32, (inner, LANES), 1),
        1.0,
        0.0,
    )
    group_b = group.astype(BF16)
    d_step = dot(dsum[...], group_b)
    u = dot(uprod[...], group_b)
    z = dot(zprod[...], group_b)
    sums = dot(line[...], group, precision=HIGH)
    d_run = rows_t[...].T - cols + u - z
    row = lax.broadcasted_iota(jnp.int32, (size, 1), 0)
    ending = sums[1:2, :] + jnp.sum(z, axis=0, keepdims=True)
    d_run = d_run + jnp.where(row == size - 1, ending, 0.0)
    d_decay = dot(jnp.where(causal, 1.0, 0.0), d_run, precision=HIGH)
    d_raw = (d_step - jnp.exp(head_ref[0:1, :]) * d_decay) * lax.logistic(raw)
    d_raw = jnp.where(lane < heads, d_raw, 0.0)
    hgrad_ref[0:1, :] += jnp.sum(d_decay * decay, axis=0, keepdims=True)
    hgrad_ref[1:2, :] += jnp.sum(d_raw, axis=0, keepdims=True)

    @pl.when(finish)
    def _():
        hgrad_ref[2:3, :] = sums[0:1, :]

    g = dmix[...] * (sig * (1.0 + mixed * (1.0 - sig)))
    gbuf[0:size, :] = g
    wgrad_ref[KW : KW + 1, :] += jnp.sum(g, axis=0, keepdims=True)
    for k in range(KW):
        wgrad_ref[k : k + 1, :] += jnp.sum(g * xbuf[5 + k : 5 + k + size, :], axis=0, keepdims=True)
    back = taps_ref[KW - 1 : KW, :] * g
    for k in range(KW - 1):
        back = back + taps_ref[k : k + 1, :] * gbuf[3 - k : 3 - k + size, :]
    out_ref[:, :wide] = back.astype(BF16)
    out_ref[:, wide:] = d_raw.astype(BF16)


MESH = pl.DeviceIdType.MESH


def where_am_i(dp):
    d, s = lax.axis_index("dp"), lax.axis_index("seq")
    z, y = d // 2, d % 2
    x, c = s // 2, s % 2
    peers = [s + 1 - 2 * c, s + 2 - 4 * x, 3 - s]
    return d, s, z, y, x, c, peers, dp // 2


def push(src, dst, send_sem, recv_sem, d, s):
    return pltpu.make_async_remote_copy(
        src_ref=src,
        dst_ref=dst,
        send_sem=send_sem,
        recv_sem=recv_sem,
        device_id={"dp": d, "seq": s},
        device_id_type=MESH,
    )


def greet(partners):
    barrier = pltpu.get_barrier_semaphore()
    for cond, d, s in partners:

        def hello(d=d, s=s):
            pl.semaphore_signal(barrier, inc=1, device_id={"dp": d, "seq": s}, device_id_type=MESH)

        if cond is None:
            hello()
        else:
            pl.when(cond)(hello)
    count = 0
    for cond, _, _ in partners:
        count = count + (1 if cond is None else jnp.where(cond, 1, 0))
    pl.semaphore_wait(barrier, count)


class Sends:
    def __init__(self):
        self.items = []

    def start(self, cond, copy):
        if cond is None:
            copy.start()
        else:
            pl.when(cond)(copy.start)
        self.items.append((cond, copy))

    def drain(self):
        for cond, copy in self.items:
            if cond is None:
                copy.wait_send()
            else:
                pl.when(cond)(copy.wait_send)


STRIPE = DI // 16


def swapped(s):
    return 2 * (s % 2) + s // 2


def stripe_owner(block, dp):
    u = dp // 4
    return block // (4 * u) * u + block % u


def stripe_seat(block, dp):
    return swapped(block // (dp // 4) % 4)


def stripe_block(d, s, dp):
    u = dp // 4
    return (d // u * 4 + swapped(s)) * u + d % u


def forward_chunk(heads, first, rest_ref, taps_ref, head_ref, ssd_ref, mem_ref, xbuf, mem):
    size = rest_ref.shape[0]
    wide = taps_ref.shape[1]
    inner = heads * P_SIZE

    @pl.when(first)
    def _():
        xbuf[0:8, :] = jnp.zeros((8, wide), F32)
        mem[...] = jnp.zeros_like(mem)

    @pl.when(jnp.logical_not(first))
    def _():
        xbuf[0:8, :] = xbuf[size : size + 8, :]

    xbuf[8 : 8 + size, :] = rest_ref[:, :wide]
    mixed, sig, _, step, _, run = chunk_parts(heads, rest_ref, xbuf, taps_ref, head_ref)
    act = mixed * sig
    run_t = run.T
    closing = run[size - 1 : size, :]
    last = jnp.exp(closing)
    left = jnp.exp(closing - run)
    grown = jnp.exp(run)
    b = act[:, inner : inner + N]
    c = act[:, inner + N :].astype(BF16)
    scores = dot(c, b.astype(BF16), NT)
    b_t = b.T.astype(BF16)
    mem_ref[...] = mem[...].astype(BF16)
    inter = dot(c, mem[...].astype(BF16))
    low = lax.broadcasted_iota(jnp.int32, (1, LANES), 1) < P_SIZE
    i = lax.broadcasted_iota(jnp.int32, (size, size), 0)
    j = lax.broadcasted_iota(jnp.int32, (size, size), 1)
    causal = i >= j
    for p in range(heads // 2):
        at = slice(p * LANES, (p + 1) * LANES)
        v = act[:, at]
        xv = pick(step, p, low) * v
        y = pick(head_ref[2:3, :], p, low) * v + pick(grown, p, low) * inter[:, at]
        for e in range(2):
            h = 2 * p + e
            gap = run[:, h : h + 1] - run_t[h : h + 1, :]
            w = (scores * jnp.exp(jnp.where(causal, gap, FAR))).astype(BF16)
            mine = jnp.where(low if e == 0 else jnp.logical_not(low), xv, 0.0).astype(BF16)
            y = y + dot(w, mine)
        ssd_ref[:, at] = y
        xc = (pick(left, p, low) * xv).astype(BF16)
        mem[:, at] = mem[:, at] * pick(last, p, low) + dot(b_t, xc)


def hop(v, size):
    return sum(jnp.where(v >= q * size, 1, 0) for q in range(1, 4))


def head_kernel(
    dp,
    heads,
    proj_ref,
    cw_ref,
    cb_ref,
    ng_ref,
    gg_ref,
    ph_ref,
    tok_ref,
    cot_ref,
    block_ref,
    normed_hbm,
    turned_hbm,
    proj_hbm,
    ssd_hbm,
    mem_hbm,
    gates_hbm,
    rest_hbm,
    gate_hbm,
    out_hbm,
    cot_hbm,
    taps_ref,
    gain_ref,
    gated_ref,
    head_ref,
    line,
    small_stage,
    val_stage,
    half_stage,
    gate_stage,
    small_all,
    val_in,
    half_in,
    gate_in,
    w_val,
    w_half,
    w_other,
    w_tail,
    w_gate,
    out_shard,
    tok,
    flipped,
    proj,
    ssd,
    gates,
    memory,
    xbuf,
    mem,
    l_sem,
    o_sem,
    f_sem,
    p_sem,
    g_sem,
    a_send,
    a_recv,
    z_send,
    z_recv,
    y_send,
    y_recv,
    t_send,
    t_recv,
):
    d, s, z, y, x, c, peers, deep = where_am_i(dp)
    tp, rows = val_stage.shape[:2]
    micro, part, width = tok_ref.shape
    total = dp * tp
    inner = heads * P_SIZE
    wide = inner + 2 * N
    chan, gpiece = cw_ref.shape[1], gg_ref.shape[1]
    up, down, far = d + 2, d - 2, d + 1 - 2 * y
    me = d * tp + s
    to_d, to_s, turned = stripe_owner(me, dp), stripe_seat(me, dp), stripe_block(d, s, dp)
    from_d, from_s = turned // tp, turned % tp
    moves = turned != me

    triple = HEADS // 16
    line[...] = jnp.zeros_like(line)
    line[0:KW, 0:chan] = cw_ref[...].astype(F32)
    line[KW : KW + 1, 0:chan] = cb_ref[...].astype(F32)
    line[KW + 1 : KW + 2, 0:rows] = ng_ref[...].astype(F32)
    line[KW + 2 : KW + 3, 0:gpiece] = gg_ref[...].astype(F32)
    raw = proj_ref[:, 2 * DI + 2 * N :]
    for b in range(4):
        seat = 2 * (b % 2) + b // 2
        for k in range(4):
            to, at = k * STRIPE, (4 * k + b) * STRIPE
            gate_stage[seat, :, to : to + STRIPE] = proj_ref[:, at : at + STRIPE]
            val_stage[seat, :, to : to + STRIPE] = proj_ref[:, DI + at : DI + at + STRIPE]
        at = 2 * DI + N * (seat % 2)
        half_stage[seat] = proj_ref[:, at : at + N]
        v = lax.broadcasted_iota(jnp.int32, (16, HEADS), 0)
        g = lax.broadcasted_iota(jnp.int32, (16, HEADS), 1)
        hit = jnp.logical_and(v < heads, g == v + 3 * triple * hop(v, triple) + triple * b)
        line[16:32, 0:rows] = dot(jnp.where(hit, 1.0, 0.0).astype(BF16), raw, NT)
        small_stage[seat] = line[...].astype(BF16)
    v = lax.broadcasted_iota(jnp.int32, (HEADS, LANES), 1)
    g = lax.broadcasted_iota(jnp.int32, (HEADS, LANES), 0)
    hit = jnp.logical_and(v < heads, g == v + 3 * triple * hop(v, triple) + triple * swapped(s))
    head_ref[...] = dot(ph_ref[...], jnp.where(hit, 1.0, 0.0), precision=HIGH)

    greet(
        [(None, d, p) for p in peers]
        + [(None, far, s), (z < deep - 1, up, s), (z > 0, down, s)]
        + [(moves, to_d, to_s), (moves, from_d, from_s)]
    )
    sends = Sends()

    def arrive(dst, sem):
        push(dst, dst, sem, sem, d, peers[0]).wait_recv()

    def mine(ref, k):
        return ref.at[:, pl.ds(k * part, part), :]

    def exchange(a, stage, target):
        for r, p in enumerate(peers):
            sends.start(
                None, push(stage.at[p], target(s), a_send.at[a, r], a_recv.at[a, r], d, p)
            )

    def exchanged(a, target):
        for r, p in enumerate(peers):
            arrive(target(p), a_recv.at[a, r])

    exchange(0, small_stage, lambda k: small_all.at[d, k])
    exchange(1, half_stage, lambda k: half_in.at[k])
    exchange(2, val_stage, lambda k: val_in.at[k])
    exchange(3, gate_stage, lambda k: gate_in.at[k])
    sends.start(moves, push(block_ref, out_shard, t_send.at[2], t_recv.at[2], to_d, to_s))
    sends.start(None, push(tok_ref, mine(tok, s), t_send.at[0], t_recv.at[0], d, peers[1]))
    sends.start(None, push(tok_ref, mine(tok, s), t_send.at[1], t_recv.at[1], d, peers[0]))
    sends.start(None, push(cot_ref, mine(cot_hbm, s), t_send.at[3], t_recv.at[3], d, peers[1]))
    sends.start(None, push(cot_ref, mine(cot_hbm, s), t_send.at[4], t_recv.at[4], d, peers[0]))
    saves = []

    def save(src, dst):
        copy = pltpu.make_async_copy(src, dst, l_sem.at[len(saves)])
        copy.start()
        saves.append(copy)

    save(cot_ref, mine(cot_hbm, s))
    small_all[d, s] = small_stage[s]
    half_in[s] = half_stage[s]
    val_in[s] = val_stage[s]
    gate_in[s] = gate_stage[s]
    tok[:, pl.ds(pl.multiple_of(s * part, part), part), :] = tok_ref[...]

    @pl.when(jnp.logical_not(moves))
    def _():
        out_shard[...] = block_ref[...]

    def begin(a, shard, dst):
        block = dst.at[d]
        sends.start(z < deep - 1, push(shard, block, z_send.at[a, 0, 0], z_recv.at[a, 0, 0], up, s))
        sends.start(z > 0, push(shard, block, z_send.at[a, 1, 0], z_recv.at[a, 1, 0], down, s))
        sends.start(None, push(shard, block, y_send.at[a, 0, 0], y_recv.at[a, 0, 0], far, s))

    def plan(a, dst, t):
        steps = []
        for way in range(2):
            here = (z >= t) if way == 0 else (z + t <= deep - 1)
            more = jnp.logical_and(here, (z < deep - 1) if way == 0 else (z > 0))
            at = jnp.clip(d - 2 * t if way == 0 else d + 2 * t, 0, dp - 1)
            block = dst.at[at]
            got = z_recv.at[a, way, t - 1]
            on = []
            if t < deep - 1:
                nxt = up if way == 0 else down
                on.append(
                    (more, push(block, block, z_send.at[a, way, t], z_recv.at[a, way, t], nxt, s))
                )
            on.append(
                (here, push(block, block, y_send.at[a, way, t], y_recv.at[a, way, t], far, s))
            )
            steps.append((here, push(block, block, got, got, d, peers[0]), on))
        return steps

    def run(steps):
        for here, wait, on in steps:
            pl.when(here)(wait.wait_recv)
            for cond, copy in on:
                pl.when(cond)(copy.start)

    def remember(steps):
        for _, _, on in steps:
            sends.items.extend(on)

    def relay(a, dst, t):
        steps = plan(a, dst, t)
        run(steps)
        remember(steps)

    def landed(a, dst):
        arrive(dst.at[far], y_recv.at[a, 0, 0])
        for t in range(1, deep):
            for way in range(2):
                here = (z >= t) if way == 0 else (z + t <= deep - 1)
                at = jnp.clip(far - 2 * t if way == 0 else far + 2 * t, 0, dp - 1)
                pl.when(here)(functools.partial(arrive, dst.at[at], y_recv.at[a, way, t]))

    def shard_of(a, pieces, dst):
        exchanged(a, lambda p: pieces.at[p])
        for k in range(tp):
            dst[d, k * rows : (k + 1) * rows, :] = pieces[k]
        begin(a, dst.at[d], dst)

    exchanged(0, lambda p: small_all.at[d, p])
    begin(0, small_all.at[d], small_all)
    shard_of(1, half_in, w_half)
    shard_of(2, val_in, w_val)
    for t in range(1, deep):
        relay(0, small_all, t)
        relay(1, w_half, t)
        relay(2, w_val, t)
    shard_of(3, gate_in, w_gate)
    pl.when(moves)(functools.partial(arrive, out_shard, t_recv.at[2]))
    begin(4, out_shard, out_hbm)
    save(out_shard, out_hbm.at[d])

    landed(0, small_all)

    def one_hot(columns, index, k, length):
        lane = lax.broadcasted_iota(jnp.int32, (LANES, columns), 1)
        at = lax.broadcasted_iota(jnp.int32, (LANES, columns), 0)
        hit = jnp.logical_and(at < length, index(lane) == k * length + at)
        return jnp.where(hit, 1.0, 0.0).astype(BF16)

    taps_ref[...] = jnp.zeros_like(taps_ref)
    gain_ref[...] = jnp.zeros_like(gain_ref)
    gated_ref[...] = jnp.zeros_like(gated_ref)

    def striped(v):
        return v + 3 * STRIPE * hop(v, STRIPE) + STRIPE * swapped(s)

    def lay_out(dd, carry):
        for kk in range(tp):
            k = dd * tp + kk
            values = small_all[dd, kk, 0:16, :]
            chans = one_hot(wide, lambda v: jnp.where(v < inner, striped(v), v - inner + DI), k, chan)
            taps_ref[...] += dot(values, chans)[:8]
            gain_ref[...] += dot(values, one_hot(width, lambda v: v, k, rows))
            gated_ref[...] += dot(values, one_hot(inner, striped, k, gpiece))
            turned = jnp.concatenate(
                [small_all[dd, kk, 16:32, :].astype(F32), jnp.zeros((LANES - 16, LANES), F32)], axis=0
            ).T
            w_tail[dd, kk * rows : (kk + 1) * rows, 2 * N :] = turned[:rows].astype(BF16)
        return carry

    lax.fori_loop(0, dp, lay_out, 0)
    landed(1, w_half)
    sends.start(None, push(w_half, w_other, t_send.at[6], t_recv.at[6], d, peers[0]))
    landed(2, w_val)
    save(w_val, rest_hbm.at[:, :, pl.ds(0, inner)])
    arrive(w_other, t_recv.at[6])

    def both_halves(dd, carry):
        w_tail[dd, :, pl.ds(pl.multiple_of(c * N, N), N)] = w_half[dd]
        w_tail[dd, :, pl.ds(pl.multiple_of((1 - c) * N, N), N)] = w_other[dd]
        return carry

    lax.fori_loop(0, dp, both_halves, 0)
    save(w_tail, rest_hbm.at[:, :, pl.ds(inner, w_tail.shape[2])])
    arrive(mine(tok, peers[1]), t_recv.at[0])
    block = mine(tok, peers[1])
    hand = push(block, block, t_send.at[5], t_recv.at[5], d, peers[0])
    hand.start()
    relay(3, w_gate, 1)
    relay(4, out_hbm, 1)
    arrive(mine(tok, peers[0]), t_recv.at[1])
    arrive(mine(tok, peers[2]), t_recv.at[5])
    hand.wait_send()

    tasks = [(a, ref, t) for t in range(2, deep) for a, ref in ((3, w_gate), (4, out_hbm))]
    chunks = micro * tp
    when = {}
    for n, task in enumerate(tasks):
        when.setdefault(min(n * 4 // len(tasks), chunks - 1), []).append(plan(*task))
    for plans in when.values():
        for steps in plans:
            remember(steps)

    def columns(i):
        return pl.ds(pl.multiple_of(i * part, part), part)

    def chunk(i, carry):
        m, k = i // tp, i % tp
        lines = pl.ds(pl.multiple_of(k * part, part), part)
        h = tok[m, lines, :].astype(F32)
        r = lax.rsqrt(jnp.mean(h * h, axis=-1, keepdims=True) + EPSILON)
        value = h * r * gain_ref[5:6, :]
        tok[m, lines, :] = value.astype(BF16)
        flipped[i] = value.T.astype(BF16)
        proj[i, :, 0:inner] = dot(tok[m, lines, :], w_val[...].reshape(width, inner))
        proj[i, :, inner:] = dot(tok[m, lines, :], w_tail[...].reshape(width, w_tail.shape[2]))
        forward_chunk(
            heads, k == 0, proj.at[i], taps_ref, head_ref, ssd.at[i], memory.at[i], xbuf, mem
        )
        pltpu.make_async_copy(tok.at[m, lines, :], normed_hbm.at[m, lines, :], o_sem.at[i]).start()
        pltpu.make_async_copy(flipped.at[i], turned_hbm.at[:, columns(i)], f_sem.at[i]).start()
        pltpu.make_async_copy(proj.at[i], proj_hbm.at[i], p_sem.at[i]).start()
        for n, plans in when.items():

            @pl.when(i == n)
            def _():
                for steps in plans:
                    run(steps)

        return carry

    lax.fori_loop(0, chunks, chunk, 0)
    save(ssd, ssd_hbm)
    save(memory, mem_hbm)
    arrive(mine(cot_hbm, peers[1]), t_recv.at[3])
    block = mine(cot_hbm, peers[1])
    sends.start(None, push(block, block, t_send.at[7], t_recv.at[7], d, peers[0]))
    landed(3, w_gate)
    save(w_gate, gate_hbm)

    def gating(i, carry):
        m, k = i // tp, i % tp
        lines = pl.ds(pl.multiple_of(k * part, part), part)
        gates[i] = dot(tok[m, lines, :], w_gate[...].reshape(width, inner))
        pltpu.make_async_copy(gates.at[i], gates_hbm.at[i], g_sem.at[i]).start()
        return carry

    lax.fori_loop(0, chunks, gating, 0)
    landed(4, out_hbm)
    arrive(mine(cot_hbm, peers[0]), t_recv.at[4])
    arrive(mine(cot_hbm, peers[2]), t_recv.at[7])

    def saved(i, carry):
        m, k = i // tp, i % tp
        lines = pl.ds(pl.multiple_of(k * part, part), part)
        pltpu.make_async_copy(tok.at[m, lines, :], normed_hbm.at[m, lines, :], o_sem.at[i]).wait()
        pltpu.make_async_copy(flipped.at[i], turned_hbm.at[:, columns(i)], f_sem.at[i]).wait()
        pltpu.make_async_copy(proj.at[i], proj_hbm.at[i], p_sem.at[i]).wait()
        pltpu.make_async_copy(gates.at[i], gates_hbm.at[i], g_sem.at[i]).wait()
        return carry

    lax.fori_loop(0, chunks, saved, 0)
    for copy in saves:
        copy.wait()
    sends.drain()


def head(in_proj, conv_weight, conv_bias, norm_gain, gated_gain, per_head, tokens, cotangent, out_proj, dp, tp):
    rows = in_proj.shape[0]
    heads = HEADS // tp
    inner = heads * P_SIZE
    full = inner + 2 * N + LANES
    micro, part, width = tokens.shape
    deep = dp // 2
    chunks = micro * tp
    block = tp * rows
    dma = pltpu.SemaphoreType.DMA
    vmem = pl.BlockSpec(memory_space=pltpu.VMEM)
    hbm = pl.BlockSpec(memory_space=pl.ANY)
    wide = inner + 2 * N

    def shape(*dims, kind=BF16):
        return jax.ShapeDtypeStruct(dims, kind)

    def room(*dims, kind=BF16):
        return pltpu.VMEM(dims, kind)

    return pl.pallas_call(
        functools.partial(head_kernel, dp, heads),
        in_specs=[vmem] * 9,
        out_specs=[hbm] * 10 + [vmem] * 4,
        out_shape=[
            shape(micro, tp * part, width),
            shape(width, chunks * part),
            shape(chunks, part, full, kind=F32),
            shape(chunks, part, inner, kind=F32),
            shape(chunks, N, inner),
            shape(chunks, part, inner, kind=F32),
            shape(dp, block, full),
            shape(dp, block, inner),
            shape(dp, out_proj.shape[0], width),
            shape(micro, tp * part, width),
            shape(8, wide, kind=F32),
            shape(16, width, kind=F32),
            shape(16, inner, kind=F32),
            shape(8, LANES, kind=F32),
        ],
        scratch_shapes=[
            room(32, LANES, kind=F32),
            room(tp, 32, LANES),
            room(tp, rows, inner),
            room(tp, rows, N),
            room(tp, rows, inner),
            room(dp, tp, 32, LANES),
            room(tp, rows, inner),
            room(tp, rows, N),
            room(tp, rows, inner),
            room(dp, block, inner),
            room(dp, block, N),
            room(dp, block, N),
            room(dp, block, 2 * N + LANES),
            room(dp, block, inner),
            room(*out_proj.shape),
            room(micro, tp * part, width),
            room(chunks, width, part),
            room(chunks, part, full, kind=F32),
            room(chunks, part, inner, kind=F32),
            room(chunks, part, inner, kind=F32),
            room(chunks, N, inner),
            room(part + 8, wide, kind=F32),
            room(N, inner, kind=F32),
            dma((8,)),
            dma((chunks,)),
            dma((chunks,)),
            dma((chunks,)),
            dma((chunks,)),
            dma((4, 3)),
            dma((4, 3)),
            dma((5, 2, deep - 1)),
            dma((5, 2, deep - 1)),
            dma((5, 2, deep)),
            dma((5, 2, deep)),
            dma((8,)),
            dma((8,)),
        ],
        compiler_params=pltpu.CompilerParams(
            collective_id=1, has_side_effects=True, vmem_limit_bytes=62 * 2**20
        ),
        cost_estimate=pl.CostEstimate(flops=10**11, bytes_accessed=5 * 10**7, transcendentals=0),
        name="gather_and_mix",
    )(in_proj, conv_weight, conv_bias, norm_gain, gated_gain, per_head, tokens, cotangent, out_proj)


class OwnerSum:
    def __init__(self, where, sends, source, mine, ybuf, zbuf, final, sems, theirs_ref=None):
        self.where, self.sends = where, sends
        self.mine, self.ybuf, self.zbuf, self.final = mine, ybuf, zbuf, final
        d, s, z, y, _, _, _, deep = where
        self.load_sem, y_send, self.y_recv, z_send, self.z_recv = sems
        lower = z < deep // 2

        def place(j):
            low = jnp.where(j > z, deep - 1 - j, deep - 1 - z + j)
            high = jnp.where(j < z, j, z + deep - 1 - j)
            return jnp.where(j == z, deep - 1, jnp.where(lower, low, high))

        def turn(k):
            low = jnp.where(k < deep - 1 - z, deep - 1 - k, k - (deep - 1 - z))
            high = jnp.where(k < z, k, deep - 1 - (k - z))
            return jnp.where(lower, low, high) if k < deep - 1 else z

        self.order = [turn(k) for k in range(deep)]
        self.y_items, self.loads = [], []
        for k, j in enumerate(self.order):
            theirs = source.at[j * 2 + 1 - y] if theirs_ref is None else theirs_ref.at[k]
            copy = push(theirs, ybuf.at[k], y_send.at[k], self.y_recv.at[k], d + 1 - 2 * y, s)
            self.y_items.append((None, copy))
            if theirs_ref is None:
                own = source.at[j * 2 + y]
                self.loads.append(pltpu.make_async_copy(own, mine.at[k], self.load_sem.at[k]))
        self.z_items = []
        for t in range(deep - 1):
            ways = []
            for way in range(2):
                depth = z if way == 0 else deep - 1 - z
                j = deep - 1 - t + z if way == 0 else t + z - deep + 1
                k = place(jnp.clip(j, 0, deep - 1))
                nxt = d + 2 if way == 0 else d - 2
                dst, ss, rs = zbuf.at[way, t], z_send.at[way, t], self.z_recv.at[way, t]
                first = (depth == 0, push(ybuf.at[k], dst, ss, rs, nxt, s))
                later = None
                if t > 0:
                    cond = jnp.logical_and(depth > 0, depth <= t)
                    later = (cond, push(zbuf.at[way, t - 1], dst, ss, rs, nxt, s))
                ways.append((k, first, later))
            self.z_items.append(ways)
        sends.items.extend(self.y_items)
        for ways in self.z_items:
            for _, first, later in ways:
                sends.items.append(first)
                if later is not None:
                    sends.items.append(later)

    def arrive(self, ref, sem):
        d, s = self.where[:2]
        push(ref, ref, sem, sem, d, self.where[6][0]).wait_recv()

    def begin(self):
        for _, copy in self.y_items:
            copy.start()
        for copy in self.loads:
            copy.start()

    def each(self, work):
        if self.mine.ndim == 4:
            count, cut = self.mine.shape[1], lambda i: i
        else:
            count, cut = self.mine.shape[1] // 16, lambda i: pl.ds(pl.multiple_of(i * 16, 16), 16)
        lax.fori_loop(0, count, lambda i, carry: (work(cut(i)), carry)[1], 0)

    def add(self, k):
        if self.loads:
            self.loads[k].wait()
        self.arrive(self.ybuf.at[k], self.y_recv.at[k])
        ybuf, mine = self.ybuf, self.mine

        def work(i):
            ybuf[k, i] = (ybuf[k, i].astype(F32) + mine[k, i].astype(F32)).astype(BF16)

        self.each(work)

    def send(self, t):
        zbuf, ybuf = self.zbuf, self.ybuf
        for way, (k, first, later) in enumerate(self.z_items[t]):
            pl.when(first[0])(first[1].start)
            if later is None:
                continue

            @pl.when(later[0])
            def _():
                self.arrive(zbuf.at[way, t - 1], self.z_recv.at[way, t - 1])

                def work(i):
                    zbuf[way, t - 1, i] = (
                        zbuf[way, t - 1, i].astype(F32) + ybuf[k, i].astype(F32)
                    ).astype(BF16)

                self.each(work)
                later[1].start()

    def finish(self):
        z, deep = self.where[2], self.where[7]
        zbuf, ybuf, final = self.zbuf, self.ybuf, self.final
        for way in range(2):
            depth = z if way == 0 else deep - 1 - z
            pl.when(depth > 0)(
                functools.partial(self.arrive, zbuf.at[way, deep - 2], self.z_recv.at[way, deep - 2])
            )

        def work(ways, i):
            total = ybuf[deep - 1, i].astype(F32)
            for way in ways:
                total = total + zbuf[way, deep - 2, i].astype(F32)
            final[i] = total.astype(BF16)

        for cond, ways in (
            (z == 0, (1,)),
            (z == deep - 1, (0,)),
            (jnp.logical_and(z > 0, z < deep - 1), (0, 1)),
        ):
            pl.when(cond)(functools.partial(self.each, functools.partial(work, ways)))


def middle_kernel(
    dp,
    heads,
    rest_ref,
    prev_ref,
    dy_ref,
    mem_ref,
    taps_ref,
    head_ref,
    part_hbm,
    gout_hbm,
    ggate_hbm,
    tok_hbm,
    out_ref,
    wgrad_ref,
    hgrad_ref,
    own_hbm,
    gout_out,
    ggate_out,
    xbuf,
    gbuf,
    adj,
    dmix,
    dsum,
    uprod,
    zprod,
    rows_t,
    line,
    o_mine,
    o_y,
    o_z,
    o_final,
    g_mine,
    g_y,
    g_z,
    g_final,
    own,
    core_buf,
    x_buf,
    tok,
    result,
    o_load,
    o_ysend,
    o_yrecv,
    o_zsend,
    o_zrecv,
    g_load,
    g_ysend,
    g_yrecv,
    g_zsend,
    g_zrecv,
    b_load,
    c_send,
    c_recv,
    m_send,
    m_recv,
    a_send,
    a_recv,
):
    where = where_am_i(dp)
    d, s, z, y, x, c, peers, deep = where
    micro, part, width = result.shape
    step = pl.program_id(0) * pl.num_programs(1) + pl.program_id(1)
    tp = ggate_hbm.shape[1]
    me = d * tp + s
    turned = stripe_block(d, s, dp)
    moves = turned != me
    to_d, to_s = turned // tp, turned % tp
    from_d, from_s = stripe_owner(me, dp), stripe_seat(me, dp)
    sends = Sends()
    gout = OwnerSum(
        where, sends, gout_hbm, o_mine, o_y, o_z, o_final, (o_load, o_ysend, o_yrecv, o_zsend, o_zrecv)
    )
    ggate = OwnerSum(
        where, sends, ggate_hbm, g_mine, g_y, g_z, g_final, (g_load, g_ysend, g_yrecv, g_zsend, g_zrecv)
    )

    def chunk(k):
        return part_hbm.at[:, pl.ds(k * part, part), :]

    cores, loads = [], []
    for q, xx in enumerate((1 - x, x)):
        cores.append(
            push(chunk(xx * 2 + 1 - c), core_buf.at[q], c_send.at[q], c_recv.at[q], d, peers[0])
        )
        loads.append(pltpu.make_async_copy(chunk(xx * 2 + c), own.at[q], b_load.at[q]))
    across = push(core_buf.at[0], x_buf, m_send.at[0], m_recv.at[0], d, peers[1])
    turning = push(o_final, gout_out, m_send.at[1], m_recv.at[1], to_d, to_s)
    staying = pltpu.make_async_copy(o_final, gout_out, b_load.at[2])
    swaps = [
        push(g_final.at[p], ggate_out.at[s], a_send.at[r], a_recv.at[r], d, p)
        for r, p in enumerate(peers)
    ]
    kept = pltpu.make_async_copy(g_final.at[s], ggate_out.at[s], b_load.at[3])
    saved = pltpu.make_async_copy(result, own_hbm, b_load.at[4])
    loads.append(pltpu.make_async_copy(tok_hbm, tok, b_load.at[5]))
    for copy in cores + [across] + swaps:
        sends.items.append((None, copy))
    sends.items.append((moves, turning))
    span = 16

    def by_rows(work):
        def one(i, carry):
            m, row = i // (part // span), (i % (part // span)) * span
            work(m, pl.ds(pl.multiple_of(row, span), span))
            return carry

        lax.fori_loop(0, micro * (part // span), one, 0)

    def start():
        greet(
            [(None, d, p) for p in peers]
            + [(None, d + 1 - 2 * y, s), (z < deep - 1, d + 2, s), (z > 0, d - 2, s)]
            + [(moves, to_d, to_s), (moves, from_d, from_s)]
        )
        for copy in cores + loads:
            copy.start()
        gout.begin()
        ggate.begin()

    def pass_on():
        loads[0].wait()
        cores[0].wait_recv()

        def work(m, rows):
            core_buf[0, m, rows, :] = (
                core_buf[0, m, rows, :].astype(F32) + own[0, m, rows, :].astype(F32)
            ).astype(BF16)

        by_rows(work)
        across.start()

    def collect():
        loads[1].wait()
        loads[2].wait()
        cores[1].wait_recv()
        across.wait_recv()

        def work(m, rows):
            result[m, rows, :] = (
                core_buf[1, m, rows, :].astype(F32)
                + own[1, m, rows, :].astype(F32)
                + x_buf[m, rows, :].astype(F32)
                + tok[m, rows, :].astype(F32)
            ).astype(BF16)

        by_rows(work)
        saved.start()

    def hand_over():
        gout.finish()
        pl.when(moves)(turning.start)
        pl.when(jnp.logical_not(moves))(staying.start)

    def last():
        ggate.finish()
        for copy in swaps:
            copy.start()
        kept.start()
        pl.when(moves)(turning.wait_recv)
        pl.when(jnp.logical_not(moves))(staying.wait)
        for r, p in enumerate(peers):
            push(ggate_out.at[p], ggate_out.at[p], a_send.at[r], a_recv.at[r], d, p).wait_recv()
        kept.wait()
        saved.wait()
        sends.drain()

    stages = {}

    def at(n, task, *args):
        stages.setdefault(n, []).append(functools.partial(task, *args))

    at(0, start)
    at(1, pass_on)
    for k in range(deep):
        n = 1 + k * 3 // (deep - 1)
        at(n, gout.add, k)
        if k < deep - 1:
            at(n, gout.send, k)
    at(4, hand_over)
    at(5, ggate.add, 0)
    for k in range(deep - 1):
        n = 5 + k * 2 // (deep - 2)
        at(n, ggate.send, k)
        at(n, ggate.add, k + 1)
    at(6, collect)
    for n, tasks in stages.items():

        @pl.when(step == n)
        def _():
            for task in tasks:
                task()

    backward_kernel(
        heads,
        rest_ref,
        prev_ref,
        dy_ref,
        mem_ref,
        taps_ref,
        head_ref,
        out_ref,
        wgrad_ref,
        hgrad_ref,
        xbuf,
        gbuf,
        adj,
        dmix,
        dsum,
        uprod,
        zprod,
        rows_t,
        line,
    )
    pl.when(step == pl.num_programs(0) * pl.num_programs(1) - 1)(last)


def middle(rest, dy, memory, taps, head, partial, gout, ggate, tokens, dp, tp, heads, micro):
    count, full = rest.shape
    wide = taps.shape[1]
    inner = heads * P_SIZE
    _, length, width = partial.shape
    part = length // tp
    chunks = length // part
    deep = dp // 2
    dma = pltpu.SemaphoreType.DMA
    hbm = pl.BlockSpec(memory_space=pl.ANY)
    gout = gout.reshape(dp, 2, -1, width)

    def at(m, c):
        return m * chunks + chunks - 1 - c

    def sums(block):
        kinds = [(deep,), (deep,), (2, deep - 1), ()]
        return [pltpu.VMEM(kind + block, BF16) for kind in kinds]

    sems = [dma((deep,))] * 3 + [dma((2, deep - 1))] * 2
    out = pl.pallas_call(
        functools.partial(middle_kernel, dp, heads),
        grid=(micro, chunks),
        in_specs=[
            pl.BlockSpec((part, full), lambda m, c: (at(m, c), 0)),
            pl.BlockSpec((8, full), lambda m, c: (jnp.maximum(at(m, c) * (part // 8) - 1, 0), 0)),
            pl.BlockSpec((part, inner), lambda m, c: (at(m, c), 0)),
            pl.BlockSpec((1, N, inner), lambda m, c: (at(m, c), 0, 0)),
            pl.BlockSpec((8, wide), lambda m, c: (0, 0)),
            pl.BlockSpec((8, LANES), lambda m, c: (0, 0)),
            hbm,
            hbm,
            hbm,
            hbm,
        ],
        out_specs=[
            pl.BlockSpec((part, full), lambda m, c: (at(m, c), 0)),
            pl.BlockSpec((8, wide), lambda m, c: (0, 0)),
            pl.BlockSpec((8, LANES), lambda m, c: (0, 0)),
            hbm,
            hbm,
            hbm,
        ],
        out_shape=[
            jax.ShapeDtypeStruct((count, full), BF16),
            jax.ShapeDtypeStruct((8, wide), F32),
            jax.ShapeDtypeStruct((8, LANES), F32),
            jax.ShapeDtypeStruct((micro, part, width), BF16),
            jax.ShapeDtypeStruct(gout.shape[1:], BF16),
            jax.ShapeDtypeStruct(ggate.shape[1:], BF16),
        ],
        scratch_shapes=[
            pltpu.VMEM((part + 8, wide), F32),
            pltpu.VMEM((part + 8, wide), F32),
            pltpu.VMEM((N, inner), F32),
            pltpu.VMEM((part, wide), F32),
            pltpu.VMEM((part, inner), BF16),
            pltpu.VMEM((part, inner), BF16),
            pltpu.VMEM((part, inner), BF16),
            pltpu.VMEM((LANES, part), F32),
            pltpu.VMEM((8, inner), F32),
        ]
        + sums(gout.shape[1:])
        + sums(ggate.shape[1:])
        + [
            pltpu.VMEM((2, micro, part, width), BF16),
            pltpu.VMEM((2, micro, part, width), BF16),
            pltpu.VMEM((micro, part, width), BF16),
            pltpu.VMEM((micro, part, width), BF16),
            pltpu.VMEM((micro, part, width), BF16),
        ]
        + sems
        + sems
        + [dma((6,)), dma((2,)), dma((2,)), dma((2,)), dma((2,)), dma((3,)), dma((3,))],
        compiler_params=pltpu.CompilerParams(
            dimension_semantics=("arbitrary", "arbitrary"),
            collective_id=4,
            has_side_effects=True,
            vmem_limit_bytes=62 * 2**20,
        ),
        cost_estimate=pl.CostEstimate(flops=7 * 10**10, bytes_accessed=4 * 10**7, transcendentals=0),
        name="mixer_backward_and_sums",
    )(rest, rest, dy, memory, taps, head, partial, gout, ggate, tokens)
    rest_grad, wgrad, hgrad, own, gout, ggate = out
    return rest_grad, wgrad, hgrad, own, gout.reshape(-1, width), ggate


def gating_kernel(
    dp,
    ssd_hbm,
    gate_hbm,
    cot_hbm,
    out_hbm,
    turned_hbm,
    gain_ref,
    grad_ssd_hbm,
    grad_gate_hbm,
    part_hbm,
    gout_hbm,
    ggate_hbm,
    ssd,
    gate,
    cot,
    w_out,
    turned,
    weighed,
    shaped_t,
    grad_gate,
    partial,
    gout,
    ggate,
    stats,
    held,
    l_sem,
    c_sem,
    s_sem,
    g_sem,
    p_sem,
    o_sem,
    send,
    recv,
):
    d, s, *_, peers, _ = where_am_i(dp)
    chunks, part, inner = ssd.shape
    width = cot.shape[2]
    count = chunks * part

    def loads(i):
        return [
            pltpu.make_async_copy(cot_hbm.at[i], cot.at[i], c_sem.at[0, i]),
            pltpu.make_async_copy(ssd_hbm.at[i], ssd.at[i], c_sem.at[1, i]),
            pltpu.make_async_copy(gate_hbm.at[i], gate.at[i], c_sem.at[2, i]),
        ]

    first = pltpu.make_async_copy(out_hbm, w_out, l_sem.at[0])
    other = pltpu.make_async_copy(turned_hbm, turned, l_sem.at[1])
    first.start()
    for i in range(chunks):
        for copy in loads(i):
            copy.start()
    other.start()
    greet([(None, d, p) for p in peers])
    first.wait()

    def gated_parts(i):
        g = gate[i]
        sig = lax.logistic(g)
        act = g * sig
        return sig, act, ssd[i] * act

    def measure(i, carry):
        for copy in loads(i):
            copy.wait()
        w = dot(cot[i], w_out[...], NT) * gain_ref[KW + 2 : KW + 3, :]
        weighed[i] = w
        _, _, gated = gated_parts(i)
        lane = lax.broadcasted_iota(jnp.int32, (part, LANES), 1)
        both = jnp.where(lane == 0, jnp.sum(gated * gated, axis=1, keepdims=True), 0.0)
        both = jnp.where(lane == 1, jnp.sum(w * gated, axis=1, keepdims=True), both)
        stats[i] = both.T[:8, :]
        return carry

    lax.fori_loop(0, chunks, measure, 0)
    copies = [push(stats, held.at[r], send.at[r], recv.at[r], d, p) for r, p in enumerate(peers)]
    for copy in copies:
        copy.start()
    for copy in copies:
        copy.wait()

    def out_copies(i):
        return [
            pltpu.make_async_copy(weighed.at[i], grad_ssd_hbm.at[i], s_sem.at[i]),
            pltpu.make_async_copy(grad_gate.at[i], grad_gate_hbm.at[i], g_sem.at[i]),
            pltpu.make_async_copy(partial.at[i], part_hbm.at[i], p_sem.at[i]),
        ]

    def columns(i):
        return pl.ds(pl.multiple_of(i * part, part), part)

    def shape_chunk(i, carry):
        sums = (stats[i] + held[0, i]) + (held[1, i] + held[2, i])
        sums = jnp.concatenate([sums, jnp.zeros((LANES - 8, part), F32)], axis=0).T
        q = lax.rsqrt(sums[:, 0:1] / DI + EPSILON)
        pull = q * q * (sums[:, 1:2] / DI)
        sig, act, gated = gated_parts(i)
        value = gated * q * gain_ref[KW + 2 : KW + 3, :]
        shaped_t[:, columns(i)] = value.T.astype(BF16)
        partial[i] = dot(value.astype(BF16), w_out[...]).astype(BF16)
        grad = q * (weighed[i] - gated * pull)
        grad_gate[i] = (grad * ssd[i] * (sig + act * (1.0 - sig))).astype(BF16)
        weighed[i] = grad * act
        for copy in out_copies(i):
            copy.start()
        return carry

    lax.fori_loop(0, chunks, shape_chunk, 0)
    other.wait()
    high, across = min(384, inner), min(512, width)

    def out_tile(i, carry):
        a = pl.ds(pl.multiple_of(i // (width // across) * high, high), high)
        b = pl.ds(pl.multiple_of(i % (width // across) * across, across), across)
        gout[a, b] = dot(shaped_t[a, :], cot[:, :, b].reshape(count, across)).astype(BF16)
        return carry

    lax.fori_loop(0, (inner // high) * (width // across), out_tile, 0)
    save_out = pltpu.make_async_copy(gout, gout_hbm, o_sem.at[0])
    save_out.start()

    def gate_tile(i, carry):
        a = pl.ds(pl.multiple_of(i // 2 * across, across), across)
        b = pl.ds(pl.multiple_of(i % 2 * (inner // 2), inner // 2), inner // 2)
        ggate[a, b] = dot(turned[a, :], grad_gate[:, :, b].reshape(count, inner // 2)).astype(BF16)
        return carry

    lax.fori_loop(0, (width // across) * 2, gate_tile, 0)
    save_gate = pltpu.make_async_copy(ggate, ggate_hbm, o_sem.at[1])
    save_gate.start()

    def saved(i, carry):
        for copy in out_copies(i):
            copy.wait()
        return carry

    lax.fori_loop(0, chunks, saved, 0)
    save_out.wait()
    save_gate.wait()


def gating(ssd, gate, cot, w_out, normed_t, gains, dp):
    chunks, part, inner = ssd.shape
    width, count = normed_t.shape
    cot = cot.reshape(chunks, part, width)
    dma = pltpu.SemaphoreType.DMA
    vmem = pl.BlockSpec(memory_space=pltpu.VMEM)
    hbm = pl.BlockSpec(memory_space=pl.ANY)

    def shape(*dims, kind=BF16):
        return jax.ShapeDtypeStruct(dims, kind)

    def room(*dims, kind=BF16):
        return pltpu.VMEM(dims, kind)

    return pl.pallas_call(
        functools.partial(gating_kernel, dp),
        in_specs=[hbm] * 5 + [vmem],
        out_specs=[hbm] * 5,
        out_shape=[
            shape(chunks, part, inner, kind=F32),
            shape(chunks, part, inner),
            shape(chunks, part, width),
            shape(inner, width),
            shape(width, inner),
        ],
        scratch_shapes=[
            room(chunks, part, inner, kind=F32),
            room(chunks, part, inner, kind=F32),
            room(chunks, part, width),
            room(inner, width),
            room(width, count),
            room(chunks, part, inner, kind=F32),
            room(inner, count),
            room(chunks, part, inner),
            room(chunks, part, width),
            room(inner, width),
            room(width, inner),
            room(chunks, 8, part, kind=F32),
            room(3, chunks, 8, part, kind=F32),
            dma((2,)),
            dma((3, chunks)),
            dma((chunks,)),
            dma((chunks,)),
            dma((chunks,)),
            dma((2,)),
            dma((3,)),
            dma((3,)),
        ],
        compiler_params=pltpu.CompilerParams(
            collective_id=2, has_side_effects=True, vmem_limit_bytes=63 * 2**20
        ),
        cost_estimate=pl.CostEstimate(flops=3 * 10**10, bytes_accessed=5 * 10**7, transcendentals=0),
        name="gating_and_gradients",
    )(ssd, gate, cot, w_out, normed_t, gains)


def tail_kernel(
    dp,
    normed_hbm,
    rows_hbm,
    gates_hbm,
    w_rest_hbm,
    w_gate_hbm,
    tok_hbm,
    cot_hbm,
    gate_hbm,
    gout_hbm,
    proj_ref,
    block_ref,
    gain_ref,
    small_ref,
    tokens_ref,
    grad_ref,
    dots_ref,
    gout_ref,
    gdots_ref,
    taps_ref,
    bias_ref,
    heads_ref,
    out_ref,
    own_ref,
    sums_ref,
    tok,
    cot,
    gate_in,
    gout,
    normed,
    rows_ref,
    gates_ref,
    w_rest,
    w_gate,
    tile,
    wtile,
    theirs,
    mine,
    ybuf,
    zbuf,
    final,
    handed,
    core_buf,
    core_out,
    x_buf,
    x_out,
    s_buf,
    l_sem,
    n_sem,
    y_send,
    y_recv,
    z_send,
    z_recv,
    a_send,
    a_recv,
    c_send,
    c_recv,
    x_send,
    x_recv,
    s_send,
    s_recv,
):
    where = where_am_i(dp)
    d, s, z, y, x, c, peers, deep = where
    tp, rows = out_ref.shape[:2]
    block = tp * rows
    micro, part, width = own_ref.shape
    full = rows_ref.shape[1]
    bits = dp.bit_length() - 1
    partners = []
    for k in range(bits):
        step = 2**k
        bit = (d // step) % 2
        partners.append(d + step - 2 * step * bit)
    sends = Sends()
    total = OwnerSum(
        where,
        sends,
        None,
        mine,
        ybuf,
        zbuf,
        final,
        (None, y_send, y_recv, z_send, z_recv),
        theirs,
    )
    loads = [
        pltpu.make_async_copy(src, dst, l_sem.at[k])
        for k, (src, dst) in enumerate(
            (
                (rows_hbm, rows_ref),
                (w_rest_hbm, w_rest),
                (gates_hbm, gates_ref),
                (w_gate_hbm, w_gate),
                (tok_hbm, tok),
                (cot_hbm, cot),
                (gate_hbm, gate_in),
                (gout_hbm, gout),
            )
        )
    ]
    fetches = []
    for k in range(deep):
        lines = pl.ds(pl.multiple_of(total.order[k] * 2 * block, 2 * block), 2 * block)
        fetches.append(pltpu.make_async_copy(normed_hbm.at[lines, :], normed.at[k], n_sem.at[k]))
    for copy in loads + fetches:
        copy.start()
    greet(
        [(None, d, p) for p in peers]
        + [(None, d + 1 - 2 * y, s), (z < deep - 1, d + 2, s), (z > 0, d - 2, s)]
        + [(None, partners[k], s) for k in range(2, bits)]
    )

    def arrive(dst, sem):
        push(dst, dst, sem, sem, d, peers[0]).wait_recv()

    sums_ref[0] = small_ref[...]
    sends.start(None, push(small_ref, s_buf.at[0], s_send.at[0], s_recv.at[0], partners[0], s))

    def each(count, work):
        lax.fori_loop(0, count, lambda i, carry: (work(i), carry)[1], 0)

    across = width // tile.shape[1]
    span = wtile.shape[1]

    def product(owner, use):
        def work(i):
            m, n = i // across, i % across
            row = pl.multiple_of((m * tp + owner) * part, part)
            col = pl.multiple_of(n * tile.shape[1], tile.shape[1])
            lines = pl.ds(col, tile.shape[1])
            tile[...] = dot(rows_ref[pl.ds(row, part), :], w_rest[lines, :], NT) + dot(
                gates_ref[pl.ds(row, part), :], w_gate[lines, :], NT
            )
            use(m, lines)

        each(micro * across, work)

    def weight(k):
        fetches[k].wait()

        def work(n):
            cols = pl.ds(pl.multiple_of(n * span, span), span)
            wtile[...] = dot(normed[k], rows_ref[:, cols])
            far = pl.ds(pl.multiple_of((1 - y) * block, block), block)
            near = pl.ds(pl.multiple_of(y * block, block), block)
            theirs[k, :, cols] = wtile[far, :].astype(BF16)
            mine[k, :, cols] = wtile[near, :].astype(BF16)

        each(full // span, work)
        total.y_items[k][1].start()

    def doubling(k):
        arrive(s_buf.at[k], s_recv.at[k])
        sums_ref[k + 1] = sums_ref[k] + s_buf[k]
        if k + 1 < bits:
            src = sums_ref.at[k + 1]
            sends.start(
                None, push(src, s_buf.at[k + 1], s_send.at[k + 1], s_recv.at[k + 1], partners[k + 1], s)
            )

    def to_core(q):
        def use(m, lines):
            core_out[q, m, :, lines] = tile[...].astype(BF16)

        return use

    def to_chip(m, lines):
        x_out[m, :, lines] = (tile[...] + core_buf[0, m, :, lines].astype(F32)).astype(BF16)

    def keep(m, lines):
        own_ref[m, :, lines] = tile[...] + core_buf[1, m, :, lines].astype(F32)

    for copy in loads[:4]:
        copy.wait()
    product((1 - x) * 2 + 1 - c, to_core(0))
    sends.start(
        None, push(core_out.at[0], core_buf.at[0], c_send.at[0], c_recv.at[0], d, peers[0])
    )
    weight(0)
    arrive(core_buf.at[0], c_recv.at[0])
    product((1 - x) * 2 + c, to_chip)
    sends.start(None, push(x_out, x_buf, x_send.at[0], x_recv.at[0], d, peers[1]))
    weight(1)
    total.add(0)
    total.send(0)
    doubling(0)
    for k in range(2, deep):
        weight(k)
    total.add(1)
    total.send(1)
    doubling(1)
    product(x * 2 + 1 - c, to_core(1))
    sends.start(
        None, push(core_out.at[1], core_buf.at[1], c_send.at[1], c_recv.at[1], d, peers[0])
    )
    for k in range(2, deep - 1):
        total.add(k)
        total.send(k)
        if k < bits:
            doubling(k)
    arrive(core_buf.at[1], c_recv.at[1])
    product(s, keep)
    for k in range(deep - 1, bits):
        doubling(k)
    for r, p in enumerate(peers):
        src, dst = sums_ref.at[bits], sums_ref.at[bits + 1 + s]
        sends.start(None, push(src, dst, s_send.at[bits + r], s_recv.at[bits + r], d, p))
    sums_ref[bits + 1 + s] = sums_ref[bits]
    for copy in loads[4:]:
        copy.wait()
    inner = gate_in.shape[2]
    wide = inner + 2 * N
    heads = inner // P_SIZE
    triple = HEADS // 16
    for b in range(4):
        seat = 2 * (b % 2) + b // 2
        for k in range(4):
            at = (4 * k + b) * STRIPE
            grad_ref[:, at : at + STRIPE] = gate_in[seat, :, k * STRIPE : (k + 1) * STRIPE].astype(F32)
    gout_ref[...] = gout[...].astype(F32)
    gdots_ref[...] = jnp.sum(gout_ref[...] * block_ref[...].astype(F32), axis=1, keepdims=True)
    for r, p in enumerate(peers):
        arrive(sums_ref.at[bits + 1 + p], s_recv.at[bits + r])
    chan = taps_ref.shape[1]
    convs = jnp.zeros((8, chan), F32)
    per_head = jnp.zeros((8, HEADS), F32)
    v = lax.broadcasted_iota(jnp.int32, (wide, chan), 0)
    g = lax.broadcasted_iota(jnp.int32, (wide, chan), 1) + chan * (d * tp + s)
    lane = lax.broadcasted_iota(jnp.int32, (LANES, HEADS), 0)
    head = lax.broadcasted_iota(jnp.int32, (LANES, HEADS), 1)
    place = []
    for p in range(tp):
        b = 2 * (p % 2) + p // 2
        from_v = jnp.where(v < inner, v + 3 * STRIPE * hop(v, STRIPE) + STRIPE * b, v - inner + DI)
        sums = sums_ref[bits + 1 + p]
        convs = convs + dot(sums[:, :wide], jnp.where(from_v == g, 1.0, 0.0), precision=HIGH)
        hit = jnp.logical_and(lane < heads, head == lane + 3 * triple * hop(lane, triple) + triple * b)
        place.append(jnp.where(hit, 1.0, 0.0))
        per_head = per_head + dot(sums[:, wide:], place[p], precision=HIGH)
    taps_ref[...] = convs[:KW]
    bias_ref[...] = convs[KW : KW + 1]
    heads_ref[...] = per_head
    total.add(deep - 1)
    total.finish()
    for p in range(tp):
        handed[p] = final[p * rows : (p + 1) * rows, :]
    for r, p in enumerate(peers):
        sends.start(None, push(handed.at[p], out_ref.at[s], a_send.at[r], a_recv.at[r], d, p))
    out_ref[s] = handed[s]

    arrive(x_buf, x_recv.at[0])

    def last(i):
        m, row = i // (part // 16), (i % (part // 16)) * 16
        lines = pl.ds(pl.multiple_of(row, 16), 16)
        h = tok[m, lines, :].astype(F32)
        r = lax.rsqrt(jnp.mean(h * h, axis=-1, keepdims=True) + EPSILON)
        n = h * r
        grad = (own_ref[m, lines, :] + x_buf[m, lines, :].astype(F32)) * gain_ref[KW + 1 : KW + 2, :]
        grad = grad - n * jnp.mean(grad * n, axis=-1, keepdims=True)
        tokens_ref[m, lines, :] = (cot[m, lines, :].astype(F32) + r * grad).astype(BF16)

    each(micro * (part // 16), last)
    for r, p in enumerate(peers):
        arrive(out_ref.at[p], a_recv.at[r])
    both = jnp.zeros((rows, 2 * N), F32)
    steps = jnp.zeros((rows, HEADS), F32)
    for b in range(4):
        seat = 2 * (b % 2) + b // 2
        for k in range(4):
            at = DI + (4 * k + b) * STRIPE
            piece = out_ref[seat, :, k * STRIPE : (k + 1) * STRIPE]
            grad_ref[:, at : at + STRIPE] = piece.astype(F32)
        both = both + out_ref[seat, :, inner:wide].astype(F32)
        steps = steps + dot(out_ref[seat, :, wide:], place[seat].astype(BF16))
    grad_ref[:, 2 * DI : 2 * DI + 2 * N] = both
    grad_ref[:, 2 * DI + 2 * N :] = steps
    dots_ref[...] = jnp.sum(grad_ref[...] * proj_ref[...].astype(F32), axis=1, keepdims=True)
    sends.drain()


def tail(
    normed_t, rows_grad, gates_grad, w_rest, w_gate, tokens, cotangent, gate_in, gout, in_proj, out_proj, gains, small, chan, dp
):
    width, count = normed_t.shape
    micro = tokens.shape[0]
    tp = gate_in.shape[0]
    full = rows_grad.shape[1]
    rows = width // dp // tp
    part = count // micro // tp
    deep = dp // 2
    bits = dp.bit_length() - 1
    block = tp * rows
    dma = pltpu.SemaphoreType.DMA
    vmem = pl.BlockSpec(memory_space=pltpu.VMEM)
    hbm = pl.BlockSpec(memory_space=pl.ANY)
    return pl.pallas_call(
        functools.partial(tail_kernel, dp),
        in_specs=[hbm] * 9 + [vmem] * 4,
        out_specs=[vmem] * 8,
        out_shape=[
            jax.ShapeDtypeStruct(tokens.shape, BF16),
            jax.ShapeDtypeStruct(in_proj.shape, F32),
            jax.ShapeDtypeStruct((rows, 1), F32),
            jax.ShapeDtypeStruct(gout.shape, F32),
            jax.ShapeDtypeStruct((gout.shape[0], 1), F32),
            jax.ShapeDtypeStruct((KW, chan), F32),
            jax.ShapeDtypeStruct((1, chan), F32),
            jax.ShapeDtypeStruct((8, HEADS), F32),
        ],
        scratch_shapes=[
            pltpu.VMEM((tp, rows, full), BF16),
            pltpu.VMEM((micro, part, width), F32),
            pltpu.VMEM((bits + 1 + tp,) + small.shape, F32),
            pltpu.VMEM(tokens.shape, BF16),
            pltpu.VMEM(tokens.shape, BF16),
            pltpu.VMEM(gate_in.shape, BF16),
            pltpu.VMEM(gout.shape, BF16),
            pltpu.VMEM((deep, 2 * block, count), BF16),
            pltpu.VMEM(rows_grad.shape, BF16),
            pltpu.VMEM(gates_grad.shape, BF16),
            pltpu.VMEM(w_rest.shape, BF16),
            pltpu.VMEM(w_gate.shape, BF16),
            pltpu.VMEM((part, min(width, 512)), F32),
            pltpu.VMEM((2 * block, 384 if full % 384 == 0 else LANES), F32),
            pltpu.VMEM((deep, block, full), BF16),
            pltpu.VMEM((deep, block, full), BF16),
            pltpu.VMEM((deep, block, full), BF16),
            pltpu.VMEM((2, deep - 1, block, full), BF16),
            pltpu.VMEM((block, full), BF16),
            pltpu.VMEM((tp, rows, full), BF16),
            pltpu.VMEM((2, micro, part, width), BF16),
            pltpu.VMEM((2, micro, part, width), BF16),
            pltpu.VMEM((micro, part, width), BF16),
            pltpu.VMEM((micro, part, width), BF16),
            pltpu.VMEM((bits,) + small.shape, F32),
            dma((8,)),
            dma((deep,)),
            dma((deep,)),
            dma((deep,)),
            dma((2, deep - 1)),
            dma((2, deep - 1)),
            dma((3,)),
            dma((3,)),
            dma((2,)),
            dma((2,)),
            dma((1,)),
            dma((1,)),
            dma((bits + 3,)),
            dma((bits + 3,)),
        ],
        compiler_params=pltpu.CompilerParams(
            collective_id=3, has_side_effects=True, vmem_limit_bytes=62 * 2**20
        ),
        cost_estimate=pl.CostEstimate(flops=6 * 10**10, bytes_accessed=3 * 10**7, transcendentals=0),
        name="gradients_to_owners",
    )(
        normed_t,
        rows_grad,
        gates_grad,
        w_rest,
        w_gate,
        tokens,
        cotangent,
        gate_in,
        gout,
        in_proj,
        out_proj,
        gains,
        small,
    )


def body(
    tokens,
    in_proj,
    conv_weight,
    conv_bias,
    decay_log,
    step_bias,
    skip_gain,
    norm_gain,
    gated_gain,
    out_proj,
    cotangent,
):
    dp, tp = lax.axis_size("dp"), lax.axis_size("seq")
    s = lax.axis_index("seq")
    micro, part, width = tokens.shape
    heads = HEADS // tp
    inner = heads * P_SIZE
    rows = in_proj.shape[0]
    length = part * tp
    count = micro * length
    wide = inner + 2 * N
    chan = conv_bias.shape[0]

    per_head = jnp.pad(jnp.stack([decay_log, step_bias, skip_gain]), ((0, 5), (0, 0)))
    (
        normed,
        normed_t,
        proj_rest,
        ssd,
        memory,
        gate,
        w_rest,
        w_gate,
        w_out,
        cot,
        taps,
        gains,
        g_gated,
        per_head,
    ) = head(
        in_proj,
        conv_weight,
        conv_bias[None],
        norm_gain[None],
        gated_gain[None],
        per_head,
        tokens,
        cotangent,
        out_proj,
        dp,
        tp,
    )
    proj_rest = proj_rest.reshape(count, wide + LANES)
    w_rest = w_rest.reshape(width, wide + LANES)
    w_gate = w_gate.reshape(width, inner)
    grad_ssd, grad_gate, out_part, grad_out, gate_in = gating(
        ssd, gate, cot, w_out.reshape(inner, width), normed_t, g_gated, dp
    )
    grad_ssd = grad_ssd.reshape(count, inner)
    grad_gate = grad_gate.reshape(count, inner)
    grad_rest, wgrad, hgrad, out_part, grad_out, gate_in = middle(
        proj_rest,
        grad_ssd,
        memory,
        taps,
        per_head,
        out_part.reshape(micro, length, width),
        grad_out.reshape(dp, -1, width),
        gate_in.reshape(dp, tp, rows, inner),
        tokens,
        dp,
        tp,
        heads,
        micro,
    )
    small = jnp.concatenate([wgrad, hgrad], axis=1)
    tokens_grad, in_grad, dots, grad_out, gdots, conv_grad, bias_grad, head_grads = tail(
        normed_t,
        grad_rest,
        grad_gate,
        w_rest,
        w_gate,
        tokens,
        cotangent,
        gate_in,
        grad_out,
        in_proj,
        out_proj,
        gains,
        small,
        chan,
        dp,
    )
    return (
        out_part,
        tokens_grad,
        in_grad,
        conv_grad,
        bias_grad[0],
        head_grads[0],
        head_grads[1],
        head_grads[2],
        dots[:, 0] / norm_gain.astype(F32),
        gdots[:, 0] / gated_gain.astype(F32),
        grad_out,
    )


def solution(mesh):
    both = ("dp", "seq")
    return jax.shard_map(
        body,
        mesh=mesh,
        in_specs=(
            P("dp", "seq", None),
            P(both, None),
            P(None, both),
            P(both),
            P(),
            P(),
            P(),
            P(both),
            P(both),
            P(both, None),
            P("dp", "seq", None),
        ),
        out_specs=(
            P("dp", "seq", None),
            P("dp", "seq", None),
            P(both, None),
            P(None, both),
            P(both),
            P(),
            P(),
            P(),
            P(both),
            P(both),
            P(both, None),
        ),
        check_vma=False,
    )
```

profile of v0, /device:TPU:0, one launch (start us, length us, event | category | flops | bytes accessed | tf_op | source)
XLA Modules:
  0.0 306.1 jit_solution(14855734463193317662)
XLA Ops:
  0.6 1.3 select_maximum_fusion.ph_ref
  1.9 103.3 %gather_and_mix.1 = (bf16[2,1024,1536]{2,1,0:T(8,128)(2,1)}, bf16[1536,2048]{1,0:T(8,128)(2,1)}, f32[8,256,1152]{2,1,0:T(8,128)}, f32[8,256,768]{2,1,0:T(8,128)}...) custom-call(bf16[48,6448]{1,0:T(8,128)(2,1)} %proj_ref.3, ...), custom_call_target="tpu_custom_call" | custom-call | flops 99999997952 | bytes 50000000 | tf_op jit(solution)/shard_map/gather_and_mix/pallas_call | solution.py:702
  105.2 43.8 %gating_and_gradients.1 = (f32[8,256,768]{2,1,0:T(8,128)}, bf16[8,256,768]{2,1,0:T(8,128)(2,1)}, bf16[8,256,1536]{2,1,0:T(8,128)(2,1)}, bf16[768,1536]{1,0:T(8,128)(2,1)}, bf16[1536,768]{1,0:T(8,128)(2,1)}) custom-call(f32[8,256,768]{2,1,0:T(8,128)} %get-tuple-element.44.ssd_hbm, f32[8,256,768]{2,1,0:T(8,128)} %get-tuple-element.45.gate_hbm, ...), custom_call_target="tpu_custom_call" | custom-call | flops 30000001024 | bytes 50000000 | tf_op jit(solution)/shard_map/gating_and_gradients/pallas_call | solution.py:1348
  149.0 76.4 %mixer_backward_and_sums.1 = (bf16[2048,1152]{1,0:T(8,128)(2,1)}, f32[8,1024]{1,0:T(8,128)}, f32[8,128]{1,0:T(8,128)}, bf16[2,256,1536]{2,1,0:T(8,128)(2,1)}, bf...) custom-call(f32[2048,1152]{1,0:T(8,128)} %bitcast.30, f32[2048,1152]{1,0:T(8,128)} %bitcast.31, ...), custom_call_target="tpu_custom_call" | custom-call | flops 70000001024 | bytes 40000000 | tf_op jit(solution)/shard_map/mixer_backward_and_sums/pallas_call | solution.py:1125
  225.3 1.4 pad_maximum_fusion.small_ref
  226.7 70.0 %gradients_to_owners.1 = (bf16[2,256,1536]{2,1,0:T(8,128)(2,1)}, f32[48,6448]{1,0:T(8,128)}, f32[48,1]{1,0:T(8,128)}, f32[96,1536]{1,0:T(8,128)}, f32[96,1]{1,0:...) custom-call(bf16[1536,2048]{1,0:T(8,128)(2,1)} %get-tuple-element.48.turned_hbm.normed_hbm, ...), custom_call_target="tpu_custom_call" | custom-call | flops 60000002048 | bytes 30000000 | tf_op jit(solution)/shard_map/gradients_to_owners/pallas_call | solution.py:1688
  296.7 0.8 reduce
  297.6 0.9 reduce.1
  298.5 0.0 copy-done.5
  298.5 0.0 copy-start.1
  298.5 0.5 convert_divide_fusion
  299.1 0.0 copy-done.6
  299.1 0.5 convert_divide_fusion.1
  299.6 1.3 slice_bitcast_fusion
  300.9 0.0 copy-done
  300.9 1.1 copy.28
  302.0 0.0 copy-done.1
  302.0 1.1 copy.29
  303.2 1.0 copy.30
  304.2 0.6 copy.31
  304.8 0.0 copy-done.7
  304.8 0.5 copy.32
  305.3 0.0 copy-done.3
  305.3 0.8 copy.33
  (9 shorter events, 0.0 us)
Async XLA Ops:
  226.7 71.8 %copy-start.5 = (bf16[96]{0:T(256)(128)(2,1)S(1)}, bf16[96]{0:T(256)(128)(2,1)}, u32[]{:S(2)}) copy-start(bf16[96]{0:T(256)(128)(2,1)} %param.19) | copy-start | bytes 580
  226.7 72.3 %copy-start.6 = (bf16[48]{0:T(256)(128)(2,1)S(1)}, bf16[48]{0:T(256)(128)(2,1)}, u32[]{:S(2)}) copy-start(bf16[48]{0:T(256)(128)(2,1)} %param.18) | copy-start | bytes 292
  226.7 74.2 %copy-start = (bf16[2,256,1536]{2,1,0:T(8,128)(2,1)S(1)}, bf16[2,256,1536]{2,1,0:T(8,128)(2,1)}, u32[]{:S(2)}) copy-start(bf16[2,256,1536]{2,1,0:T(8,128)(2,1)} %get-tuple-element.89) | copy-start | bytes 4718596
  298.5 3.5 %copy-start.1 = (bf16[2,256,1536]{2,1,0:T(8,128)(2,1)S(1)}, bf16[2,256,1536]{2,1,0:T(8,128)(2,1)}, u32[]{:S(2)}) copy-start(bf16[2,256,1536]{2,1,0:T(8,128)(2,1)} %get-tuple-element.90) | copy-start | bytes 4718596
  300.9 2.3 copy-start.2
  302.0 2.2 copy-start.4
  302.0 2.8 copy-start.7
  302.0 3.3 %copy-start.3 = (f32[96,1536]{1,0:T(8,128)S(1)}, f32[96,1536]{1,0:T(8,128)}, u32[]{:S(2)}) copy-start(f32[96,1536]{1,0:T(8,128)} %get-tuple-element.99) | copy-start | bytes 1769476
where the time goes:
time: 307 us; the launch traced here: 306 us
  Pallas kernels  293 us (95%)
  local copies, waits for them, and re-layouts  6.57 us (2%)
  other arithmetic  5.47 us (2%)
    pallas_call x1, Pallas kernels, head(): pl.pallas_call(functools.partial(head_kernel, dp, heads), in_specs=[vmem]...  103 us
    pallas_call x1, Pallas kernels, middle(): pl.pallas_call(functools.partial(middle_kernel, dp, heads), grid=(micro,...  76.4 us
    pallas_call x1, Pallas kernels, tail(): pl.pallas_call(functools.partial(tail_kernel, dp), in_specs=[hbm] * 9 + [...  70 us
    pallas_call x1, Pallas kernels, gating(): pl.pallas_call(functools.partial(gating_kernel, dp), in_specs=[hbm] * 5 +...  43.8 us

commit v1 on v0

--- a/solution.py
+++ b/solution.py
@@ -513,7 +513,8 @@
 
     def run(steps):
         for here, wait, on in steps:
-            pl.when(here)(wait.wait_recv)
+            if wait is not None:
+                pl.when(here)(wait.wait_recv)
             for cond, copy in on:
                 pl.when(cond)(copy.start)
 
@@ -525,6 +526,26 @@
         steps = plan(a, dst, t)
         run(steps)
         remember(steps)
+
+    def pair(ref, t, way):
+        at = jnp.clip(z - t if way == 0 else z + t, 0, deep - 1)
+        return ref.at[pl.ds(2 * at, 2)]
+
+    def plan_pair(a, ref, t):
+        steps = []
+        for way in range(2):
+            here = (z >= t) if way == 0 else (z + t <= deep - 1)
+            more = jnp.logical_and(here, (z < deep - 1) if way == 0 else (z > 0))
+            block = pair(ref, t, way)
+            on = []
+            if t < deep - 1:
+                nxt = up if way == 0 else down
+                on.append(
+                    (more, push(block, block, z_send.at[a, way, t], z_recv.at[a, way, t], nxt, s))
+                )
+            got = z_recv.at[a, way, max(t - 1, 0)]
+            steps.append((here, push(block, block, got, got, d, peers[0]) if t else None, on))
+        return steps
 
     def landed(a, dst):
         arrive(dst.at[far], y_recv.at[a, 0, 0])
@@ -548,7 +569,15 @@
         relay(0, small_all, t)
         relay(1, w_half, t)
         relay(2, w_val, t)
-    shard_of(3, gate_in, w_gate)
+    exchanged(3, lambda p: gate_in.at[p])
+    for k in range(tp):
+        w_gate[d, k * rows : (k + 1) * rows, :] = gate_in[k]
+    cut = max(tp * rows // 32, 1) * 16
+    lower = w_gate.at[:, pl.ds(0, cut), :]
+    upper = w_gate.at[:, pl.ds(cut, tp * rows - cut), :]
+    crossing = push(upper.at[d], upper.at[d], y_send.at[5, 0, 0], y_recv.at[5, 0, 0], far, s)
+    sends.start(None, crossing)
+    begin(3, lower.at[d], lower)
     pl.when(moves)(functools.partial(arrive, out_shard, t_recv.at[2]))
     begin(4, out_shard, out_hbm)
     save(out_shard, out_hbm.at[d])
@@ -600,17 +629,25 @@
     block = mine(tok, peers[1])
     hand = push(block, block, t_send.at[5], t_recv.at[5], d, peers[0])
     hand.start()
-    relay(3, w_gate, 1)
+    crossing.wait_recv()
+    steps = plan_pair(5, upper, 0)
+    run(steps)
+    remember(steps)
+    relay(3, lower, 1)
     relay(4, out_hbm, 1)
     arrive(mine(tok, peers[0]), t_recv.at[1])
     arrive(mine(tok, peers[2]), t_recv.at[5])
     hand.wait_send()
 
-    tasks = [(a, ref, t) for t in range(2, deep) for a, ref in ((3, w_gate), (4, out_hbm))]
+    tasks = []
+    for t in range(2, deep):
+        tasks += [(plan, 3, lower, t), (plan_pair, 5, upper, t - 1), (plan, 4, out_hbm, t)]
+    tasks.append((plan_pair, 5, upper, deep - 1))
     chunks = micro * tp
     when = {}
     for n, task in enumerate(tasks):
-        when.setdefault(min(n * 4 // len(tasks), chunks - 1), []).append(plan(*task))
+        steps = task[0](*task[1:])
+        when.setdefault(min(n * 6 // len(tasks), chunks - 1), []).append(steps)
     for plans in when.values():
         for steps in plans:
             remember(steps)
@@ -649,7 +686,7 @@
     arrive(mine(cot_hbm, peers[1]), t_recv.at[3])
     block = mine(cot_hbm, peers[1])
     sends.start(None, push(block, block, t_send.at[7], t_recv.at[7], d, peers[0]))
-    landed(3, w_gate)
+    landed(3, lower)
     save(w_gate, gate_hbm)
 
     def gating(i, carry):
@@ -750,10 +787,10 @@
             dma((chunks,)),
             dma((4, 3)),
             dma((4, 3)),
-            dma((5, 2, deep - 1)),
-            dma((5, 2, deep - 1)),
-            dma((5, 2, deep)),
-            dma((5, 2, deep)),
+            dma((6, 2, deep - 1)),
+            dma((6, 2, deep - 1)),
+            dma((6, 2, deep)),
+            dma((6, 2, deep)),
             dma((8,)),
             dma((8,)),
         ],
@@ -1424,6 +1461,10 @@
     w_gate,
     tile,
     wtile,
+    btile,
+    b_own,
+    b_out,
+    b_in,
     theirs,
     mine,
     ybuf,
@@ -1437,6 +1478,8 @@
     s_buf,
     l_sem,
     n_sem,
+    b_send,
+    b_recv,
     y_send,
     y_recv,
     z_send,
@@ -1455,7 +1498,7 @@
     tp, rows = out_ref.shape[:2]
     block = tp * rows
     micro, part, width = own_ref.shape
-    full = rows_ref.shape[1]
+    inner = gates_ref.shape[1]
     bits = dp.bit_length() - 1
     partners = []
     for k in range(bits):
@@ -1528,16 +1571,29 @@
 
     def weight(k):
         fetches[k].wait()
+        far = pl.ds(pl.multiple_of((1 - y) * block, block), block)
+        near = pl.ds(pl.multiple_of(y * block, block), block)
 
         def work(n):
             cols = pl.ds(pl.multiple_of(n * span, span), span)
             wtile[...] = dot(normed[k], rows_ref[:, cols])
-            far = pl.ds(pl.multiple_of((1 - y) * block, block), block)
-            near = pl.ds(pl.multiple_of(y * block, block), block)
             theirs[k, :, cols] = wtile[far, :].astype(BF16)
             mine[k, :, cols] = wtile[near, :].astype(BF16)
 
-        each(full // span, work)
+        lines = pl.ds(inner, 2 * N)
+        btile[...] = dot(normed[k], rows_ref[:, lines])
+        ours = pl.ds(pl.multiple_of(c * N, N), N)
+        b_out[k] = btile[:, pl.ds(pl.multiple_of((1 - c) * N, N), N)].astype(BF16)
+        b_own[...] = btile[:, ours]
+        swap = push(b_out.at[k], b_in.at[k], b_send.at[k], b_recv.at[k], d, peers[0])
+        sends.start(None, swap)
+        each(inner // span, work)
+        b_tail = dot(normed[k], rows_ref[:, inner + 2 * N :])
+        btile[:, N:] = b_tail
+        arrive(b_in.at[k], b_recv.at[k])
+        btile[:, 0:N] = b_own[...] + b_in[k].astype(F32)
+        theirs[k, :, inner:] = btile[far, :].astype(BF16)
+        mine[k, :, inner:] = btile[near, :].astype(BF16)
         total.y_items[k][1].start()
 
     def doubling(k):
@@ -1599,7 +1655,6 @@
     sums_ref[bits + 1 + s] = sums_ref[bits]
     for copy in loads[4:]:
         copy.wait()
-    inner = gate_in.shape[2]
     wide = inner + 2 * N
     heads = inner // P_SIZE
     triple = HEADS // 16
@@ -1654,7 +1709,7 @@
     each(micro * (part // 16), last)
     for r, p in enumerate(peers):
         arrive(out_ref.at[p], a_recv.at[r])
-    both = jnp.zeros((rows, 2 * N), F32)
+    both = [jnp.zeros((rows, N), F32), jnp.zeros((rows, N), F32)]
     steps = jnp.zeros((rows, HEADS), F32)
     for b in range(4):
         seat = 2 * (b % 2) + b // 2
@@ -1662,9 +1717,10 @@
             at = DI + (4 * k + b) * STRIPE
             piece = out_ref[seat, :, k * STRIPE : (k + 1) * STRIPE]
             grad_ref[:, at : at + STRIPE] = piece.astype(F32)
-        both = both + out_ref[seat, :, inner:wide].astype(F32)
-        steps = steps + dot(out_ref[seat, :, wide:], place[seat].astype(BF16))
-    grad_ref[:, 2 * DI : 2 * DI + 2 * N] = both
+        both[seat % 2] = both[seat % 2] + out_ref[seat, :, inner : inner + N].astype(F32)
+        steps = steps + dot(out_ref[seat, :, inner + N :], place[seat].astype(BF16))
+    grad_ref[:, 2 * DI : 2 * DI + N] = both[0]
+    grad_ref[:, 2 * DI + N : 2 * DI + 2 * N] = both[1]
     grad_ref[:, 2 * DI + 2 * N :] = steps
     dots_ref[...] = jnp.sum(grad_ref[...] * proj_ref[...].astype(F32), axis=1, keepdims=True)
     sends.drain()
@@ -1676,7 +1732,7 @@
     width, count = normed_t.shape
     micro = tokens.shape[0]
     tp = gate_in.shape[0]
-    full = rows_grad.shape[1]
+    full = gates_grad.shape[1] + N + LANES
     rows = width // dp // tp
     part = count // micro // tp
     deep = dp // 2
@@ -1713,7 +1769,11 @@
             pltpu.VMEM(w_rest.shape, BF16),
             pltpu.VMEM(w_gate.shape, BF16),
             pltpu.VMEM((part, min(width, 512)), F32),
-            pltpu.VMEM((2 * block, 384 if full % 384 == 0 else LANES), F32),
+            pltpu.VMEM((2 * block, 384), F32),
+            pltpu.VMEM((2 * block, 2 * N), F32),
+            pltpu.VMEM((2 * block, N), F32),
+            pltpu.VMEM((deep, 2 * block, N), BF16),
+            pltpu.VMEM((deep, 2 * block, N), BF16),
             pltpu.VMEM((deep, block, full), BF16),
             pltpu.VMEM((deep, block, full), BF16),
             pltpu.VMEM((deep, block, full), BF16),
@@ -1726,6 +1786,8 @@
             pltpu.VMEM((micro, part, width), BF16),
             pltpu.VMEM((bits,) + small.shape, F32),
             dma((8,)),
+            dma((deep,)),
+            dma((deep,)),
             dma((deep,)),
             dma((deep,)),
             dma((deep,)),

time: 307 us -> 308 us (level)
    pallas_call x1, Pallas kernels: 103 us -> 108 us  [head(): pl.pallas_call(functools.partial(head_kernel, dp, heads), in_specs=[vmem]...]
    pallas_call x1, Pallas kernels: 70 us -> 66.7 us  [tail(): pl.pallas_call(functools.partial(tail_kernel, dp), in_specs=[hbm] * 9 + [...]
where the time goes in v1:
time: 308 us
  Pallas kernels  295 us (96%)
  local copies, waits for them, and re-layouts  6.57 us (2%)
  other arithmetic  5.47 us (2%)
    pallas_call x1, Pallas kernels, head(): pl.pallas_call(functools.partial(head_kernel, dp, heads), in_specs=[vmem]...  108 us
    pallas_call x1, Pallas kernels, middle(): pl.pallas_call(functools.partial(middle_kernel, dp, heads), grid=(micro,...  76.6 us
    pallas_call x1, Pallas kernels, tail(): pl.pallas_call(functools.partial(tail_kernel, dp), in_specs=[hbm] * 9 + [...  66.7 us
    pallas_call x1, Pallas kernels, gating(): pl.pallas_call(functools.partial(gating_kernel, dp), in_specs=[hbm] * 5 +...  43.6 us

profile of v1, /device:TPU:0, one launch (start us, length us, event | category | flops | bytes accessed | tf_op | source)
XLA Modules:
  0.0 307.5 jit_solution(849862649527150161)
XLA Ops:
  0.6 1.3 select_maximum_fusion.ph_ref
  1.9 107.9 %gather_and_mix.1 = (bf16[2,1024,1536]{2,1,0:T(8,128)(2,1)}, bf16[1536,2048]{1,0:T(8,128)(2,1)}, f32[8,256,1152]{2,1,0:T(8,128)}, f32[8,256,768]{2,1,0:T(8,128)}...) custom-call(bf16[48,6448]{1,0:T(8,128)(2,1)} %proj_ref.3, ...), custom_call_target="tpu_custom_call" | custom-call | flops 99999997952 | bytes 50000000 | tf_op jit(solution)/shard_map/gather_and_mix/pallas_call | solution.py:739
  109.9 43.6 %gating_and_gradients.1 = (f32[8,256,768]{2,1,0:T(8,128)}, bf16[8,256,768]{2,1,0:T(8,128)(2,1)}, bf16[8,256,1536]{2,1,0:T(8,128)(2,1)}, bf16[768,1536]{1,0:T(8,128)(2,1)}, bf16[1536,768]{1,0:T(8,128)(2,1)}) custom-call(f32[8,256,768]{2,1,0:T(8,128)} %get-tuple-element.44.ssd_hbm, f32[8,256,768]{2,1,0:T(8,128)} %get-tuple-element.45.gate_hbm, ...), custom_call_target="tpu_custom_call" | custom-call | flops 30000001024 | bytes 50000000 | tf_op jit(solution)/shard_map/gating_and_gradients/pallas_call | solution.py:1385
  153.5 76.6 %mixer_backward_and_sums.1 = (bf16[2048,1152]{1,0:T(8,128)(2,1)}, f32[8,1024]{1,0:T(8,128)}, f32[8,128]{1,0:T(8,128)}, bf16[2,256,1536]{2,1,0:T(8,128)(2,1)}, bf...) custom-call(f32[2048,1152]{1,0:T(8,128)} %bitcast.30, f32[2048,1152]{1,0:T(8,128)} %bitcast.31, ...), custom_call_target="tpu_custom_call" | custom-call | flops 70000001024 | bytes 40000000 | tf_op jit(solution)/shard_map/mixer_backward_and_sums/pallas_call | solution.py:1162
  230.1 1.4 pad_maximum_fusion.small_ref
  231.5 66.7 %gradients_to_owners.1 = (bf16[2,256,1536]{2,1,0:T(8,128)(2,1)}, f32[48,6448]{1,0:T(8,128)}, f32[48,1]{1,0:T(8,128)}, f32[96,1536]{1,0:T(8,128)}, f32[96,1]{1,0:...) custom-call(bf16[1536,2048]{1,0:T(8,128)(2,1)} %get-tuple-element.48.turned_hbm.normed_hbm, ...), custom_call_target="tpu_custom_call" | custom-call | flops 60000002048 | bytes 30000000 | tf_op jit(solution)/shard_map/gradients_to_owners/pallas_call | solution.py:1744
  298.1 0.8 reduce
  299.0 0.9 reduce.1
  299.9 0.0 copy-done.5
  299.9 0.0 copy-start.1
  299.9 0.5 convert_divide_fusion
  300.5 0.0 copy-done.6
  300.5 0.5 convert_divide_fusion.1
  301.0 1.3 slice_bitcast_fusion
  302.3 0.0 copy-done
  302.3 1.1 copy.28
  303.4 0.0 copy-done.1
  303.4 1.1 copy.29
  304.6 1.0 copy.30
  305.6 0.6 copy.31
  306.2 0.0 copy-done.7
  306.2 0.5 copy.32
  306.7 0.0 copy-done.3
  306.7 0.8 copy.33
  (9 shorter events, 0.0 us)
Async XLA Ops:
  231.5 68.5 %copy-start.5 = (bf16[96]{0:T(256)(128)(2,1)S(1)}, bf16[96]{0:T(256)(128)(2,1)}, u32[]{:S(2)}) copy-start(bf16[96]{0:T(256)(128)(2,1)} %param.19) | copy-start | bytes 580
  231.5 69.0 %copy-start.6 = (bf16[48]{0:T(256)(128)(2,1)S(1)}, bf16[48]{0:T(256)(128)(2,1)}, u32[]{:S(2)}) copy-start(bf16[48]{0:T(256)(128)(2,1)} %param.18) | copy-start | bytes 292
  231.5 70.8 %copy-start = (bf16[2,256,1536]{2,1,0:T(8,128)(2,1)S(1)}, bf16[2,256,1536]{2,1,0:T(8,128)(2,1)}, u32[]{:S(2)}) copy-start(bf16[2,256,1536]{2,1,0:T(8,128)(2,1)} %get-tuple-element.89) | copy-start | bytes 4718596
  299.9 3.5 %copy-start.1 = (bf16[2,256,1536]{2,1,0:T(8,128)(2,1)S(1)}, bf16[2,256,1536]{2,1,0:T(8,128)(2,1)}, u32[]{:S(2)}) copy-start(bf16[2,256,1536]{2,1,0:T(8,128)(2,1)} %get-tuple-element.90) | copy-start | bytes 4718596
  302.3 2.3 copy-start.2
  303.4 2.2 copy-start.4
  303.4 2.8 copy-start.7
  303.4 3.3 %copy-start.3 = (f32[96,1536]{1,0:T(8,128)S(1)}, f32[96,1536]{1,0:T(8,128)}, u32[]{:S(2)}) copy-start(f32[96,1536]{1,0:T(8,128)} %get-tuple-element.99) | copy-start | bytes 1769476

commit v2 on v0

--- a/solution.py
+++ b/solution.py
@@ -40,6 +40,12 @@
     for k in range(1, KW):
         mixed = mixed + taps_ref[k : k + 1, :] * xbuf[5 + k : 5 + k + size, :]
     sig = lax.logistic(mixed)
+    return (mixed, sig) + step_parts(heads, rest_ref, taps_ref, head_ref)
+
+
+def step_parts(heads, rest_ref, taps_ref, head_ref):
+    size = rest_ref.shape[0]
+    wide = taps_ref.shape[1]
     lane = lax.broadcasted_iota(jnp.int32, (1, LANES), 1)
     raw = jnp.where(lane < heads, rest_ref[:, wide:], 0.0) + head_ref[1:2, :]
     step = jnp.maximum(raw, 0.0) + jnp.log1p(jnp.exp(-jnp.abs(raw)))
@@ -47,7 +53,7 @@
     i = lax.broadcasted_iota(jnp.int32, (size, size), 0)
     j = lax.broadcasted_iota(jnp.int32, (size, size), 1)
     run = dot(jnp.where(i >= j, 1.0, 0.0), decay, precision=HIGH)
-    return mixed, sig, raw, step, decay, run
+    return raw, step, decay, run
 
 
 def backward_kernel(
@@ -70,6 +76,8 @@
     zprod,
     rows_t,
     line,
+    acts,
+    slopes,
 ):
     size = rest_ref.shape[0]
     wide = taps_ref.shape[1]
@@ -99,16 +107,23 @@
 
     xbuf[0:8, :] = jnp.where(oldest, 0.0, prev_ref[:, :wide])
     xbuf[8 : 8 + size, :] = rest_ref[:, :wide]
-    mixed, sig, raw, step, decay, run = chunk_parts(heads, rest_ref, xbuf, taps_ref, head_ref)
-    act = mixed * sig
+    for n in range(wide // LANES):
+        at = slice(n * LANES, (n + 1) * LANES)
+        mixed = taps_ref[KW : KW + 1, at] + taps_ref[0:1, at] * xbuf[5 : 5 + size, at]
+        for k in range(1, KW):
+            mixed = mixed + taps_ref[k : k + 1, at] * xbuf[5 + k : 5 + k + size, at]
+        sig = lax.logistic(mixed)
+        acts[:, at] = mixed * sig
+        slopes[:, at] = sig * (1.0 + mixed * (1.0 - sig))
+    raw, step, decay, run = step_parts(heads, rest_ref, taps_ref, head_ref)
     run_t = run.T
     closing = run[size - 1 : size, :]
     last = jnp.exp(closing)
     left = jnp.exp(closing - run)
     grown = jnp.exp(run)
-    b = act[:, inner : inner + N].astype(BF16)
-    c = act[:, inner + N :].astype(BF16)
-    c_t = act[:, inner + N :].T.astype(BF16)
+    b = acts[:, inner : inner + N].astype(BF16)
+    c = acts[:, inner + N :].astype(BF16)
+    c_t = acts[:, inner + N :].T.astype(BF16)
     scores_t = dot(b, c, NT)
     low = lax.broadcasted_iota(jnp.int32, (1, LANES), 1) < P_SIZE
     lane = lax.broadcasted_iota(jnp.int32, (1, LANES), 1)
@@ -123,7 +138,7 @@
     cols = jnp.zeros((size, LANES), F32)
     for p in range(heads // 2):
         at = slice(p * LANES, (p + 1) * LANES)
-        v = act[:, at]
+        v = acts[:, at]
         size_p = pick(step, p, low)
         xv = size_p * v
         dy = dy_ref[:, at]
@@ -191,15 +206,18 @@
     def _():
         hgrad_ref[2:3, :] = sums[0:1, :]
 
-    g = dmix[...] * (sig * (1.0 + mixed * (1.0 - sig)))
-    gbuf[0:size, :] = g
-    wgrad_ref[KW : KW + 1, :] += jnp.sum(g, axis=0, keepdims=True)
-    for k in range(KW):
-        wgrad_ref[k : k + 1, :] += jnp.sum(g * xbuf[5 + k : 5 + k + size, :], axis=0, keepdims=True)
-    back = taps_ref[KW - 1 : KW, :] * g
-    for k in range(KW - 1):
-        back = back + taps_ref[k : k + 1, :] * gbuf[3 - k : 3 - k + size, :]
-    out_ref[:, :wide] = back.astype(BF16)
+    for n in range(wide // LANES):
+        at = slice(n * LANES, (n + 1) * LANES)
+        g = dmix[:, at] * slopes[:, at]
+        gbuf[0:size, at] = g
+        wgrad_ref[KW : KW + 1, at] += jnp.sum(g, axis=0, keepdims=True)
+        for k in range(KW):
+            lag = xbuf[5 + k : 5 + k + size, at]
+            wgrad_ref[k : k + 1, at] += jnp.sum(g * lag, axis=0, keepdims=True)
+        back = taps_ref[KW - 1 : KW, at] * g
+        for k in range(KW - 1):
+            back = back + taps_ref[k : k + 1, at] * gbuf[3 - k : 3 - k + size, at]
+        out_ref[:, at] = back.astype(BF16)
     out_ref[:, wide:] = d_raw.astype(BF16)
 
 
@@ -913,6 +931,8 @@
     zprod,
     rows_t,
     line,
+    acts,
+    slopes,
     o_mine,
     o_y,
     o_z,
@@ -1040,6 +1060,7 @@
         pl.when(jnp.logical_not(moves))(staying.start)
 
     def last():
+        ggate.add(deep - 1)
         ggate.finish()
         for copy in swaps:
             copy.start()
@@ -1059,17 +1080,16 @@
 
     at(0, start)
     at(1, pass_on)
-    for k in range(deep):
-        n = 1 + k * 3 // (deep - 1)
-        at(n, gout.add, k)
-        if k < deep - 1:
-            at(n, gout.send, k)
-    at(4, hand_over)
-    at(5, ggate.add, 0)
     for k in range(deep - 1):
-        n = 5 + k * 2 // (deep - 2)
-        at(n, ggate.send, k)
-        at(n, ggate.add, k + 1)
+        n = k * 2 // (deep - 2)
+        at(2 + n, gout.add, k)
+        at(2 + n, gout.send, k)
+    at(4, gout.add, deep - 1)
+    at(5, hand_over)
+    for k in range(deep - 1):
+        n = k * 2 // (deep - 2)
+        at(5 + n, ggate.add, k)
+        at(5 + n, ggate.send, k)
     at(6, collect)
     for n, tasks in stages.items():
 
@@ -1098,6 +1118,8 @@
         zprod,
         rows_t,
         line,
+        acts,
+        slopes,
     )
     pl.when(step == pl.num_programs(0) * pl.num_programs(1) - 1)(last)
 
@@ -1163,6 +1185,8 @@
             pltpu.VMEM((part, inner), BF16),
             pltpu.VMEM((LANES, part), F32),
             pltpu.VMEM((8, inner), F32),
+            pltpu.VMEM((part, wide), F32),
+            pltpu.VMEM((part, wide), F32),
         ]
         + sums(gout.shape[1:])
         + sums(ggate.shape[1:])
@@ -1401,7 +1425,8 @@
     proj_ref,
     block_ref,
     gain_ref,
-    small_ref,
+    wgrad_ref,
+    hgrad_ref,
     tokens_ref,
     grad_ref,
     dots_ref,
@@ -1424,6 +1449,10 @@
     w_gate,
     tile,
     wtile,
+    btile,
+    b_own,
+    b_out,
+    b_in,
     theirs,
     mine,
     ybuf,
@@ -1437,6 +1466,8 @@
     s_buf,
     l_sem,
     n_sem,
+    b_send,
+    b_recv,
     y_send,
     y_recv,
     z_send,
@@ -1455,7 +1486,7 @@
     tp, rows = out_ref.shape[:2]
     block = tp * rows
     micro, part, width = own_ref.shape
-    full = rows_ref.shape[1]
+    inner = gates_ref.shape[1]
     bits = dp.bit_length() - 1
     partners = []
     for k in range(bits):
@@ -1504,8 +1535,8 @@
     def arrive(dst, sem):
         push(dst, dst, sem, sem, d, peers[0]).wait_recv()
 
-    sums_ref[0] = small_ref[...]
-    sends.start(None, push(small_ref, s_buf.at[0], s_send.at[0], s_recv.at[0], partners[0], s))
+    sums_ref[0, :, 0 : wgrad_ref.shape[1]] = wgrad_ref[...]
+    sums_ref[0, :, wgrad_ref.shape[1] :] = hgrad_ref[...]
 
     def each(count, work):
         lax.fori_loop(0, count, lambda i, carry: (work(i), carry)[1], 0)
@@ -1528,16 +1559,29 @@
 
     def weight(k):
         fetches[k].wait()
+        far = pl.ds(pl.multiple_of((1 - y) * block, block), block)
+        near = pl.ds(pl.multiple_of(y * block, block), block)
 
         def work(n):
             cols = pl.ds(pl.multiple_of(n * span, span), span)
             wtile[...] = dot(normed[k], rows_ref[:, cols])
-            far = pl.ds(pl.multiple_of((1 - y) * block, block), block)
-            near = pl.ds(pl.multiple_of(y * block, block), block)
             theirs[k, :, cols] = wtile[far, :].astype(BF16)
             mine[k, :, cols] = wtile[near, :].astype(BF16)
 
-        each(full // span, work)
+        lines = pl.ds(inner, 2 * N)
+        btile[...] = dot(normed[k], rows_ref[:, lines])
+        ours = pl.ds(pl.multiple_of(c * N, N), N)
+        b_out[k] = btile[:, pl.ds(pl.multiple_of((1 - c) * N, N), N)].astype(BF16)
+        b_own[...] = btile[:, ours]
+        swap = push(b_out.at[k], b_in.at[k], b_send.at[k], b_recv.at[k], d, peers[0])
+        sends.start(None, swap)
+        each(inner // span, work)
+        b_tail = dot(normed[k], rows_ref[:, inner + 2 * N :])
+        btile[:, N:] = b_tail
+        arrive(b_in.at[k], b_recv.at[k])
+        btile[:, 0:N] = b_own[...] + b_in[k].astype(F32)
+        theirs[k, :, inner:] = btile[far, :].astype(BF16)
+        mine[k, :, inner:] = btile[near, :].astype(BF16)
         total.y_items[k][1].start()
 
     def doubling(k):
@@ -1563,6 +1607,8 @@
 
     for copy in loads[:4]:
         copy.wait()
+    src = sums_ref.at[0]
+    sends.start(None, push(src, s_buf.at[0], s_send.at[0], s_recv.at[0], partners[0], s))
     product((1 - x) * 2 + 1 - c, to_core(0))
     sends.start(
         None, push(core_out.at[0], core_buf.at[0], c_send.at[0], c_recv.at[0], d, peers[0])
@@ -1599,7 +1645,6 @@
     sums_ref[bits + 1 + s] = sums_ref[bits]
     for copy in loads[4:]:
         copy.wait()
-    inner = gate_in.shape[2]
     wide = inner + 2 * N
     heads = inner // P_SIZE
     triple = HEADS // 16
@@ -1654,7 +1699,7 @@
     each(micro * (part // 16), last)
     for r, p in enumerate(peers):
         arrive(out_ref.at[p], a_recv.at[r])
-    both = jnp.zeros((rows, 2 * N), F32)
+    both = [jnp.zeros((rows, N), F32), jnp.zeros((rows, N), F32)]
     steps = jnp.zeros((rows, HEADS), F32)
     for b in range(4):
         seat = 2 * (b % 2) + b // 2
@@ -1662,21 +1707,23 @@
             at = DI + (4 * k + b) * STRIPE
             piece = out_ref[seat, :, k * STRIPE : (k + 1) * STRIPE]
             grad_ref[:, at : at + STRIPE] = piece.astype(F32)
-        both = both + out_ref[seat, :, inner:wide].astype(F32)
-        steps = steps + dot(out_ref[seat, :, wide:], place[seat].astype(BF16))
-    grad_ref[:, 2 * DI : 2 * DI + 2 * N] = both
+        both[seat % 2] = both[seat % 2] + out_ref[seat, :, inner : inner + N].astype(F32)
+        steps = steps + dot(out_ref[seat, :, inner + N :], place[seat].astype(BF16))
+    grad_ref[:, 2 * DI : 2 * DI + N] = both[0]
+    grad_ref[:, 2 * DI + N : 2 * DI + 2 * N] = both[1]
     grad_ref[:, 2 * DI + 2 * N :] = steps
     dots_ref[...] = jnp.sum(grad_ref[...] * proj_ref[...].astype(F32), axis=1, keepdims=True)
     sends.drain()
 
 
 def tail(
-    normed_t, rows_grad, gates_grad, w_rest, w_gate, tokens, cotangent, gate_in, gout, in_proj, out_proj, gains, small, chan, dp
+    normed_t, rows_grad, gates_grad, w_rest, w_gate, tokens, cotangent, gate_in, gout, in_proj, out_proj, gains, wgrad, hgrad, chan, dp
 ):
     width, count = normed_t.shape
     micro = tokens.shape[0]
     tp = gate_in.shape[0]
-    full = rows_grad.shape[1]
+    small = (8, wgrad.shape[1] + hgrad.shape[1])
+    full = gates_grad.shape[1] + N + LANES
     rows = width // dp // tp
     part = count // micro // tp
     deep = dp // 2
@@ -1687,7 +1734,7 @@
     hbm = pl.BlockSpec(memory_space=pl.ANY)
     return pl.pallas_call(
         functools.partial(tail_kernel, dp),
-        in_specs=[hbm] * 9 + [vmem] * 4,
+        in_specs=[hbm] * 9 + [vmem] * 5,
         out_specs=[vmem] * 8,
         out_shape=[
             jax.ShapeDtypeStruct(tokens.shape, BF16),
@@ -1702,7 +1749,7 @@
         scratch_shapes=[
             pltpu.VMEM((tp, rows, full), BF16),
             pltpu.VMEM((micro, part, width), F32),
-            pltpu.VMEM((bits + 1 + tp,) + small.shape, F32),
+            pltpu.VMEM((bits + 1 + tp,) + small, F32),
             pltpu.VMEM(tokens.shape, BF16),
             pltpu.VMEM(tokens.shape, BF16),
             pltpu.VMEM(gate_in.shape, BF16),
@@ -1713,7 +1760,11 @@
             pltpu.VMEM(w_rest.shape, BF16),
             pltpu.VMEM(w_gate.shape, BF16),
             pltpu.VMEM((part, min(width, 512)), F32),
-            pltpu.VMEM((2 * block, 384 if full % 384 == 0 else LANES), F32),
+            pltpu.VMEM((2 * block, 384), F32),
+            pltpu.VMEM((2 * block, 2 * N), F32),
+            pltpu.VMEM((2 * block, N), F32),
+            pltpu.VMEM((deep, 2 * block, N), BF16),
+            pltpu.VMEM((deep, 2 * block, N), BF16),
             pltpu.VMEM((deep, block, full), BF16),
             pltpu.VMEM((deep, block, full), BF16),
             pltpu.VMEM((deep, block, full), BF16),
@@ -1724,8 +1775,10 @@
             pltpu.VMEM((2, micro, part, width), BF16),
             pltpu.VMEM((micro, part, width), BF16),
             pltpu.VMEM((micro, part, width), BF16),
-            pltpu.VMEM((bits,) + small.shape, F32),
+            pltpu.VMEM((bits,) + small, F32),
             dma((8,)),
+            dma((deep,)),
+            dma((deep,)),
             dma((deep,)),
             dma((deep,)),
             dma((deep,)),
@@ -1758,7 +1811,8 @@
         in_proj,
         out_proj,
         gains,
-        small,
+        wgrad,
+        hgrad,
     )
 
 
@@ -1838,7 +1892,6 @@
         heads,
         micro,
     )
-    small = jnp.concatenate([wgrad, hgrad], axis=1)
     tokens_grad, in_grad, dots, grad_out, gdots, conv_grad, bias_grad, head_grads = tail(
         normed_t,
         grad_rest,
@@ -1852,7 +1905,8 @@
         in_proj,
         out_proj,
         gains,
-        small,
+        wgrad,
+        hgrad,
         chan,
         dp,
     )

time: 307 us -> 299 us (0.974)
  Pallas kernels: 293 us -> 288 us
where the time goes in v2:
time: 299 us
  Pallas kernels  288 us (96%)
  local copies, waits for them, and re-layouts  6.58 us (2%)
  other arithmetic  4.09 us (1%)
    pallas_call x1, Pallas kernels, head(): pl.pallas_call(functools.partial(head_kernel, dp, heads), in_specs=[vmem]...  103 us
    pallas_call x1, Pallas kernels, middle(): pl.pallas_call(functools.partial(middle_kernel, dp, heads), grid=(micro,...  73.6 us
    pallas_call x1, Pallas kernels, tail(): pl.pallas_call(functools.partial(tail_kernel, dp), in_specs=[hbm] * 9 + [...  67 us
    pallas_call x1, Pallas kernels, gating(): pl.pallas_call(functools.partial(gating_kernel, dp), in_specs=[hbm] * 5 +...  43.8 us

profile of v2, /device:TPU:0, one launch (start us, length us, event | category | flops | bytes accessed | tf_op | source)
XLA Modules:
  0.0 299.0 jit_solution(7075042330814847851)
XLA Ops:
  0.6 1.3 select_maximum_fusion.ph_ref
  1.9 103.3 %gather_and_mix.1 = (bf16[2,1024,1536]{2,1,0:T(8,128)(2,1)}, bf16[1536,2048]{1,0:T(8,128)(2,1)}, f32[8,256,1152]{2,1,0:T(8,128)}, f32[8,256,768]{2,1,0:T(8,128)}...) custom-call(bf16[48,6448]{1,0:T(8,128)(2,1)} %proj_ref.3, ...), custom_call_target="tpu_custom_call" | custom-call | flops 99999997952 | bytes 50000000 | tf_op jit(solution)/shard_map/gather_and_mix/pallas_call | solution.py:720
  105.2 43.8 %gating_and_gradients.1 = (f32[8,256,768]{2,1,0:T(8,128)}, bf16[8,256,768]{2,1,0:T(8,128)(2,1)}, bf16[8,256,1536]{2,1,0:T(8,128)(2,1)}, bf16[768,1536]{1,0:T(8,128)(2,1)}, bf16[1536,768]{1,0:T(8,128)(2,1)}) custom-call(f32[8,256,768]{2,1,0:T(8,128)} %get-tuple-element.44.ssd_hbm, f32[8,256,768]{2,1,0:T(8,128)} %get-tuple-element.45.gate_hbm, ...), custom_call_target="tpu_custom_call" | custom-call | flops 30000001024 | bytes 50000000 | tf_op jit(solution)/shard_map/gating_and_gradients/pallas_call | solution.py:1372
  149.0 73.6 %mixer_backward_and_sums.1 = (bf16[2048,1152]{1,0:T(8,128)(2,1)}, f32[8,1024]{1,0:T(8,128)}, f32[8,128]{1,0:T(8,128)}, bf16[2,256,1536]{2,1,0:T(8,128)(2,1)}, bf...) custom-call(f32[2048,1152]{1,0:T(8,128)} %bitcast.30, f32[2048,1152]{1,0:T(8,128)} %bitcast.31, ...), custom_call_target="tpu_custom_call" | custom-call | flops 70000001024 | bytes 40000000 | tf_op jit(solution)/shard_map/mixer_backward_and_sums/pallas_call | solution.py:1147
  222.5 0.0 copy-start.5
  222.6 0.0 copy-start.6
  222.6 0.0 copy-start
  222.6 67.0 %gradients_to_owners.1 = (bf16[2,256,1536]{2,1,0:T(8,128)(2,1)}, f32[48,6448]{1,0:T(8,128)}, f32[48,1]{1,0:T(8,128)}, f32[96,1536]{1,0:T(8,128)}, f32[96,1]{1,0:...) custom-call(bf16[1536,2048]{1,0:T(8,128)(2,1)} %get-tuple-element.48.turned_hbm.normed_hbm, ...), custom_call_target="tpu_custom_call" | custom-call | flops 60000002048 | bytes 30000000 | tf_op jit(solution)/shard_map/gradients_to_owners/pallas_call | solution.py:1735
  289.6 0.8 reduce
  290.4 0.9 reduce.1
  291.4 0.0 copy-done.5
  291.4 0.0 copy-start.1
  291.4 0.5 convert_divide_fusion
  291.9 0.0 copy-done.6
  291.9 0.5 convert_divide_fusion.1
  292.4 1.3 slice_bitcast_fusion
  293.7 0.0 copy-done
  293.7 1.1 copy.28
  294.9 0.0 copy-done.1
  294.9 1.1 copy.29
  296.1 1.0 copy.30
  297.1 0.6 copy.31
  297.7 0.5 copy.32
  298.2 0.8 copy.33
  (8 shorter events, 0.0 us)
Async XLA Ops:
  222.5 68.8 %copy-start.5 = (bf16[96]{0:T(256)(128)(2,1)S(1)}, bf16[96]{0:T(256)(128)(2,1)}, u32[]{:S(2)}) copy-start(bf16[96]{0:T(256)(128)(2,1)} %param.19) | copy-start | bytes 580
  222.6 69.4 %copy-start.6 = (bf16[48]{0:T(256)(128)(2,1)S(1)}, bf16[48]{0:T(256)(128)(2,1)}, u32[]{:S(2)}) copy-start(bf16[48]{0:T(256)(128)(2,1)} %param.18) | copy-start | bytes 292
  222.6 71.2 %copy-start = (bf16[2,256,1536]{2,1,0:T(8,128)(2,1)S(1)}, bf16[2,256,1536]{2,1,0:T(8,128)(2,1)}, u32[]{:S(2)}) copy-start(bf16[2,256,1536]{2,1,0:T(8,128)(2,1)} %get-tuple-element.89) | copy-start | bytes 4718596
  291.4 3.5 %copy-start.1 = (bf16[2,256,1536]{2,1,0:T(8,128)(2,1)S(1)}, bf16[2,256,1536]{2,1,0:T(8,128)(2,1)}, u32[]{:S(2)}) copy-start(bf16[2,256,1536]{2,1,0:T(8,128)(2,1)} %get-tuple-element.90) | copy-start | bytes 4718596
  293.7 2.3 copy-start.2
  294.9 2.2 copy-start.4
  294.9 2.8 copy-start.7
  294.9 3.3 %copy-start.3 = (f32[96,1536]{1,0:T(8,128)S(1)}, f32[96,1536]{1,0:T(8,128)}, u32[]{:S(2)}) copy-start(f32[96,1536]{1,0:T(8,128)} %get-tuple-element.99) | copy-start | bytes 1769476

commit v3 on v2

--- a/solution.py
+++ b/solution.py
@@ -961,8 +961,6 @@
     c_recv,
     m_send,
     m_recv,
-    a_send,
-    a_recv,
 ):
     where = where_am_i(dp)
     d, s, z, y, x, c, peers, deep = where
@@ -994,14 +992,10 @@
     across = push(core_buf.at[0], x_buf, m_send.at[0], m_recv.at[0], d, peers[1])
     turning = push(o_final, gout_out, m_send.at[1], m_recv.at[1], to_d, to_s)
     staying = pltpu.make_async_copy(o_final, gout_out, b_load.at[2])
-    swaps = [
-        push(g_final.at[p], ggate_out.at[s], a_send.at[r], a_recv.at[r], d, p)
-        for r, p in enumerate(peers)
-    ]
-    kept = pltpu.make_async_copy(g_final.at[s], ggate_out.at[s], b_load.at[3])
+    kept = pltpu.make_async_copy(g_final, ggate_out, b_load.at[3])
     saved = pltpu.make_async_copy(result, own_hbm, b_load.at[4])
     loads.append(pltpu.make_async_copy(tok_hbm, tok, b_load.at[5]))
-    for copy in cores + [across] + swaps:
+    for copy in cores + [across]:
         sends.items.append((None, copy))
     sends.items.append((moves, turning))
     span = 16
@@ -1062,13 +1056,9 @@
     def last():
         ggate.add(deep - 1)
         ggate.finish()
-        for copy in swaps:
-            copy.start()
         kept.start()
         pl.when(moves)(turning.wait_recv)
         pl.when(jnp.logical_not(moves))(staying.wait)
-        for r, p in enumerate(peers):
-            push(ggate_out.at[p], ggate_out.at[p], a_send.at[r], a_recv.at[r], d, p).wait_recv()
         kept.wait()
         saved.wait()
         sends.drain()
@@ -1199,7 +1189,7 @@
         ]
         + sems
         + sems
-        + [dma((6,)), dma((2,)), dma((2,)), dma((2,)), dma((2,)), dma((3,)), dma((3,))],
+        + [dma((6,)), dma((2,)), dma((2,)), dma((2,)), dma((2,))],
         compiler_params=pltpu.CompilerParams(
             dimension_semantics=("arbitrary", "arbitrary"),
             collective_id=4,
@@ -1411,6 +1401,13 @@
     )(ssd, gate, cot, w_out, normed_t, gains)
 
 
+def as_row(column):
+    size = column.shape[0]
+    square = jnp.broadcast_to(column, (size, LANES))
+    square = jnp.concatenate([square, jnp.zeros((LANES - size, LANES), F32)], axis=0)
+    return square.T[0:1, :size]
+
+
 def tail_kernel(
     dp,
     normed_hbm,
@@ -1427,6 +1424,8 @@
     gain_ref,
     wgrad_ref,
     hgrad_ref,
+    ng_ref,
+    gg_ref,
     tokens_ref,
     grad_ref,
     dots_ref,
@@ -1468,6 +1467,8 @@
     n_sem,
     b_send,
     b_recv,
+    g_send,
+    g_recv,
     y_send,
     y_recv,
     z_send,
@@ -1515,7 +1516,7 @@
                 (w_gate_hbm, w_gate),
                 (tok_hbm, tok),
                 (cot_hbm, cot),
-                (gate_hbm, gate_in),
+                (gate_hbm.at[s], gate_in.at[s]),
                 (gout_hbm, gout),
             )
         )
@@ -1607,6 +1608,9 @@
 
     for copy in loads[:4]:
         copy.wait()
+    for r, p in enumerate(peers):
+        swap = push(gate_hbm.at[p], gate_in.at[s], g_send.at[r], g_recv.at[r], d, p)
+        sends.start(None, swap)
     src = sums_ref.at[0]
     sends.start(None, push(src, s_buf.at[0], s_send.at[0], s_recv.at[0], partners[0], s))
     product((1 - x) * 2 + 1 - c, to_core(0))
@@ -1645,6 +1649,8 @@
     sums_ref[bits + 1 + s] = sums_ref[bits]
     for copy in loads[4:]:
         copy.wait()
+    for r, p in enumerate(peers):
+        arrive(gate_in.at[p], g_recv.at[r])
     wide = inner + 2 * N
     heads = inner // P_SIZE
     triple = HEADS // 16
@@ -1654,7 +1660,8 @@
             at = (4 * k + b) * STRIPE
             grad_ref[:, at : at + STRIPE] = gate_in[seat, :, k * STRIPE : (k + 1) * STRIPE].astype(F32)
     gout_ref[...] = gout[...].astype(F32)
-    gdots_ref[...] = jnp.sum(gout_ref[...] * block_ref[...].astype(F32), axis=1, keepdims=True)
+    gsum = jnp.sum(gout_ref[...] * block_ref[...].astype(F32), axis=1, keepdims=True)
+    gdots_ref[...] = as_row(gsum) / gg_ref[...].astype(F32)
     for r, p in enumerate(peers):
         arrive(sums_ref.at[bits + 1 + p], s_recv.at[bits + r])
     chan = taps_ref.shape[1]
@@ -1712,12 +1719,13 @@
     grad_ref[:, 2 * DI : 2 * DI + N] = both[0]
     grad_ref[:, 2 * DI + N : 2 * DI + 2 * N] = both[1]
     grad_ref[:, 2 * DI + 2 * N :] = steps
-    dots_ref[...] = jnp.sum(grad_ref[...] * proj_ref[...].astype(F32), axis=1, keepdims=True)
+    nsum = jnp.sum(grad_ref[...] * proj_ref[...].astype(F32), axis=1, keepdims=True)
+    dots_ref[...] = as_row(nsum) / ng_ref[...].astype(F32)
     sends.drain()
 
 
 def tail(
-    normed_t, rows_grad, gates_grad, w_rest, w_gate, tokens, cotangent, gate_in, gout, in_proj, out_proj, gains, wgrad, hgrad, chan, dp
+    normed_t, rows_grad, gates_grad, w_rest, w_gate, tokens, cotangent, gate_in, gout, in_proj, out_proj, gains, wgrad, hgrad, norm_gain, gated_gain, chan, dp
 ):
     width, count = normed_t.shape
     micro = tokens.shape[0]
@@ -1734,14 +1742,14 @@
     hbm = pl.BlockSpec(memory_space=pl.ANY)
     return pl.pallas_call(
         functools.partial(tail_kernel, dp),
-        in_specs=[hbm] * 9 + [vmem] * 5,
+        in_specs=[hbm] * 9 + [vmem] * 7,
         out_specs=[vmem] * 8,
         out_shape=[
             jax.ShapeDtypeStruct(tokens.shape, BF16),
             jax.ShapeDtypeStruct(in_proj.shape, F32),
-            jax.ShapeDtypeStruct((rows, 1), F32),
+            jax.ShapeDtypeStruct((1, rows), F32),
             jax.ShapeDtypeStruct(gout.shape, F32),
-            jax.ShapeDtypeStruct((gout.shape[0], 1), F32),
+            jax.ShapeDtypeStruct((1, gout.shape[0]), F32),
             jax.ShapeDtypeStruct((KW, chan), F32),
             jax.ShapeDtypeStruct((1, chan), F32),
             jax.ShapeDtypeStruct((8, HEADS), F32),
@@ -1780,6 +1788,8 @@
             dma((deep,)),
             dma((deep,)),
             dma((deep,)),
+            dma((3,)),
+            dma((3,)),
             dma((deep,)),
             dma((deep,)),
             dma((2, deep - 1)),
@@ -1813,6 +1823,8 @@
         gains,
         wgrad,
         hgrad,
+        norm_gain,
+        gated_gain,
     )
 
 
@@ -1907,6 +1919,8 @@
         gains,
         wgrad,
         hgrad,
+        norm_gain[None],
+        gated_gain[None],
         chan,
         dp,
     )
@@ -1919,8 +1933,8 @@
         head_grads[0],
         head_grads[1],
         head_grads[2],
-        dots[:, 0] / norm_gain.astype(F32),
-        gdots[:, 0] / gated_gain.astype(F32),
+        dots[0],
+        gdots[0],
         grad_out,
     )
 

time: 299 us -> 294 us (0.983)
  Pallas kernels: 288 us -> 284 us
    unnamed x22 -> x24, local copies, waits for them, and re-layouts: 5.27 us -> 6.28 us
where the time goes in v3:
time: 294 us
  Pallas kernels  284 us (97%)
  local copies, waits for them, and re-layouts  7.62 us (3%)
    pallas_call x1, Pallas kernels, head(): pl.pallas_call(functools.partial(head_kernel, dp, heads), in_specs=[vmem]...  103 us
    pallas_call x1, Pallas kernels, middle(): pl.pallas_call(functools.partial(middle_kernel, dp, heads), grid=(micro,...  71 us
    pallas_call x1, Pallas kernels, tail(): pl.pallas_call(functools.partial(tail_kernel, dp), in_specs=[hbm] * 9 + [...  66.4 us
    pallas_call x1, Pallas kernels, gating(): pl.pallas_call(functools.partial(gating_kernel, dp), in_specs=[hbm] * 5 +...  43.8 us
    unnamed x24, local copies, waits for them, and re-layouts  6.28 us

profile of v3, /device:TPU:0, one launch (start us, length us, event | category | flops | bytes accessed | tf_op | source)
XLA Modules:
  0.0 294.0 jit_solution(14602459038301661949)
XLA Ops:
  0.6 1.3 select_maximum_fusion.ph_ref
  1.9 103.2 %gather_and_mix.1 = (bf16[2,1024,1536]{2,1,0:T(8,128)(2,1)}, bf16[1536,2048]{1,0:T(8,128)(2,1)}, f32[8,256,1152]{2,1,0:T(8,128)}, f32[8,256,768]{2,1,0:T(8,128)}...) custom-call(bf16[48,6448]{1,0:T(8,128)(2,1)} %proj_ref.3, ...), custom_call_target="tpu_custom_call" | custom-call | flops 99999997952 | bytes 50000000 | tf_op jit(solution)/shard_map/gather_and_mix/pallas_call | solution.py:720
  105.2 43.8 %gating_and_gradients.1 = (f32[8,256,768]{2,1,0:T(8,128)}, bf16[8,256,768]{2,1,0:T(8,128)(2,1)}, bf16[8,256,1536]{2,1,0:T(8,128)(2,1)}, bf16[768,1536]{1,0:T(8,128)(2,1)}, bf16[1536,768]{1,0:T(8,128)(2,1)}) custom-call(f32[8,256,768]{2,1,0:T(8,128)} %get-tuple-element.44.ssd_hbm, f32[8,256,768]{2,1,0:T(8,128)} %get-tuple-element.45.gate_hbm, ...), custom_call_target="tpu_custom_call" | custom-call | flops 30000001024 | bytes 50000000 | tf_op jit(solution)/shard_map/gating_and_gradients/pallas_call | solution.py:1362
  148.9 71.0 %mixer_backward_and_sums.1 = (bf16[2048,1152]{1,0:T(8,128)(2,1)}, f32[8,1024]{1,0:T(8,128)}, f32[8,128]{1,0:T(8,128)}, bf16[2,256,1536]{2,1,0:T(8,128)(2,1)}, bf...) custom-call(f32[2048,1152]{1,0:T(8,128)} %bitcast.34, f32[2048,1152]{1,0:T(8,128)} %bitcast.35, ...), custom_call_target="tpu_custom_call" | custom-call | flops 70000001024 | bytes 40000000 | tf_op jit(solution)/shard_map/mixer_backward_and_sums/pallas_call | solution.py:1137
  219.9 0.0 copy-start
  219.9 66.4 %gradients_to_owners.1 = (bf16[2,256,1536]{2,1,0:T(8,128)(2,1)}, f32[48,6448]{1,0:T(8,128)}, f32[1,48]{1,0:T(1,128)}, f32[96,1536]{1,0:T(8,128)}, f32[1,96]{1,0:...) custom-call(bf16[1536,2048]{1,0:T(8,128)(2,1)} %get-tuple-element.48.turned_hbm.normed_hbm, ...), custom_call_target="tpu_custom_call" | custom-call | flops 60000002048 | bytes 30000000 | tf_op jit(solution)/shard_map/gradients_to_owners/pallas_call | solution.py:1743
  286.4 0.0 copy-start.1
  286.4 1.3 slice_bitcast_fusion
  287.7 0.0 copy-done
  287.7 1.1 copy.30
  288.9 0.0 copy-done.1
  288.9 0.0 copy-start.5
  288.9 0.0 copy-start.3
  288.9 1.1 copy.31
  290.0 0.0 copy-done.2
  290.0 1.0 copy.32
  291.1 0.0 copy-done.4
  291.1 0.6 copy.33
  291.7 0.0 copy-done.7
  291.7 0.5 copy.34
  292.2 0.0 copy-done.6
  292.2 0.5 copy.35
  292.7 0.5 copy.36
  293.2 0.8 copy.37
  (6 shorter events, 0.0 us)
Async XLA Ops:
  219.9 67.8 %copy-start = (bf16[2,256,1536]{2,1,0:T(8,128)(2,1)S(1)}, bf16[2,256,1536]{2,1,0:T(8,128)(2,1)}, u32[]{:S(2)}) copy-start(bf16[2,256,1536]{2,1,0:T(8,128)(2,1)} %get-tuple-element.89) | copy-start | bytes 4718596
  286.4 2.5 copy-start.1
  287.7 2.3 copy-start.2
  288.9 2.2 copy-start.4
  288.9 2.8 copy-start.7
  288.9 3.3 %copy-start.6 = (f32[1,48]{1,0:T(1,128)S(1)}, f32[1,48]{1,0:T(1,128)}, u32[]{:S(2)}) copy-start(f32[1,48]{1,0:T(1,128)} %get-tuple-element.72) | copy-start | bytes 580
  288.9 3.8 %copy-start.5 = (f32[1,96]{1,0:T(1,128)S(1)}, f32[1,96]{1,0:T(1,128)}, u32[]{:S(2)}) copy-start(f32[1,96]{1,0:T(1,128)} %get-tuple-element.73) | copy-start | bytes 1156
  288.9 4.3 %copy-start.3 = (f32[96,1536]{1,0:T(8,128)S(1)}, f32[96,1536]{1,0:T(8,128)}, u32[]{:S(2)}) copy-start(f32[96,1536]{1,0:T(8,128)} %get-tuple-element.99) | copy-start | bytes 1769476

commit v4 on v3

--- a/solution.py
+++ b/solution.py
@@ -360,7 +360,9 @@
     cb_ref,
     ng_ref,
     gg_ref,
-    ph_ref,
+    dl_ref,
+    sb_ref,
+    sg_ref,
     tok_ref,
     cot_ref,
     block_ref,
@@ -451,7 +453,10 @@
     v = lax.broadcasted_iota(jnp.int32, (HEADS, LANES), 1)
     g = lax.broadcasted_iota(jnp.int32, (HEADS, LANES), 0)
     hit = jnp.logical_and(v < heads, g == v + 3 * triple * hop(v, triple) + triple * swapped(s))
-    head_ref[...] = dot(ph_ref[...], jnp.where(hit, 1.0, 0.0), precision=HIGH)
+    line[...] = jnp.zeros_like(line)
+    for k, row in enumerate((dl_ref, sb_ref, sg_ref)):
+        line[k : k + 1, 0:HEADS] = row[...]
+    head_ref[...] = dot(line[0:8, 0:HEADS], jnp.where(hit, 1.0, 0.0), precision=HIGH)
 
     greet(
         [(None, d, p) for p in peers]
@@ -628,7 +633,7 @@
     chunks = micro * tp
     when = {}
     for n, task in enumerate(tasks):
-        when.setdefault(min(n * 4 // len(tasks), chunks - 1), []).append(plan(*task))
+        when.setdefault(min(1 + n * 4 // len(tasks), chunks - 1), []).append(plan(*task))
     for plans in when.values():
         for steps in plans:
             remember(steps)
@@ -697,7 +702,7 @@
     sends.drain()
 
 
-def head(in_proj, conv_weight, conv_bias, norm_gain, gated_gain, per_head, tokens, cotangent, out_proj, dp, tp):
+def head(in_proj, conv_weight, conv_bias, norm_gain, gated_gain, d_log, s_bias, s_gain, tokens, cotangent, out_proj, dp, tp):
     rows = in_proj.shape[0]
     heads = HEADS // tp
     inner = heads * P_SIZE
@@ -719,7 +724,7 @@
 
     return pl.pallas_call(
         functools.partial(head_kernel, dp, heads),
-        in_specs=[vmem] * 9,
+        in_specs=[vmem] * 11,
         out_specs=[hbm] * 10 + [vmem] * 4,
         out_shape=[
             shape(micro, tp * part, width),
@@ -780,7 +785,19 @@
         ),
         cost_estimate=pl.CostEstimate(flops=10**11, bytes_accessed=5 * 10**7, transcendentals=0),
         name="gather_and_mix",
-    )(in_proj, conv_weight, conv_bias, norm_gain, gated_gain, per_head, tokens, cotangent, out_proj)
+    )(
+        in_proj,
+        conv_weight,
+        conv_bias,
+        norm_gain,
+        gated_gain,
+        d_log,
+        s_bias,
+        s_gain,
+        tokens,
+        cotangent,
+        out_proj,
+    )
 
 
 class OwnerSum:
@@ -1852,7 +1869,6 @@
     wide = inner + 2 * N
     chan = conv_bias.shape[0]
 
-    per_head = jnp.pad(jnp.stack([decay_log, step_bias, skip_gain]), ((0, 5), (0, 0)))
     (
         normed,
         normed_t,
@@ -1874,7 +1890,9 @@
         conv_bias[None],
         norm_gain[None],
         gated_gain[None],
-        per_head,
+        decay_log[None],
+        step_bias[None],
+        skip_gain[None],
         tokens,
         cotangent,
         out_proj,

time: 294 us -> 292 us (level)
  no operation moved by 1% of the time
where the time goes in v4:
time: 292 us
  Pallas kernels  283 us (97%)
  local copies, waits for them, and re-layouts  7.62 us (3%)
    pallas_call x1, Pallas kernels, head(): pl.pallas_call(functools.partial(head_kernel, dp, heads), in_specs=[vmem]...  101 us
    pallas_call x1, Pallas kernels, middle(): pl.pallas_call(functools.partial(middle_kernel, dp, heads), grid=(micro,...  70.5 us
    pallas_call x1, Pallas kernels, tail(): pl.pallas_call(functools.partial(tail_kernel, dp), in_specs=[hbm] * 9 + [...  66.7 us
    pallas_call x1, Pallas kernels, gating(): pl.pallas_call(functools.partial(gating_kernel, dp), in_specs=[hbm] * 5 +...  44.8 us
    unnamed x24, local copies, waits for them, and re-layouts  6.28 us

profile of v4, /device:TPU:0, one launch (start us, length us, event | category | flops | bytes accessed | tf_op | source)
XLA Modules:
  0.0 291.5 jit_solution(1017794662865803689)
XLA Ops:
  0.6 101.2 %gather_and_mix.1 = (bf16[2,1024,1536]{2,1,0:T(8,128)(2,1)}, bf16[1536,2048]{1,0:T(8,128)(2,1)}, f32[8,256,1152]{2,1,0:T(8,128)}, f32[8,256,768]{2,1,0:T(8,128)}...) custom-call(bf16[48,6448]{1,0:T(8,128)(2,1)} %proj_ref.3, ...), custom_call_target="tpu_custom_call" | custom-call | flops 99999997952 | bytes 50000000 | tf_op jit(solution)/shard_map/gather_and_mix/pallas_call | solution.py:725
  101.9 44.8 %gating_and_gradients.1 = (f32[8,256,768]{2,1,0:T(8,128)}, bf16[8,256,768]{2,1,0:T(8,128)(2,1)}, bf16[8,256,1536]{2,1,0:T(8,128)(2,1)}, bf16[768,1536]{1,0:T(8,128)(2,1)}, bf16[1536,768]{1,0:T(8,128)(2,1)}) custom-call(f32[8,256,768]{2,1,0:T(8,128)} %get-tuple-element.44.ssd_hbm, f32[8,256,768]{2,1,0:T(8,128)} %get-tuple-element.45.gate_hbm, ...), custom_call_target="tpu_custom_call" | custom-call | flops 30000001024 | bytes 50000000 | tf_op jit(solution)/shard_map/gating_and_gradients/pallas_call | solution.py:1379
  146.7 70.5 %mixer_backward_and_sums.1 = (bf16[2048,1152]{1,0:T(8,128)(2,1)}, f32[8,1024]{1,0:T(8,128)}, f32[8,128]{1,0:T(8,128)}, bf16[2,256,1536]{2,1,0:T(8,128)(2,1)}, bf...) custom-call(f32[2048,1152]{1,0:T(8,128)} %bitcast.34, f32[2048,1152]{1,0:T(8,128)} %bitcast.35, ...), custom_call_target="tpu_custom_call" | custom-call | flops 70000001024 | bytes 40000000 | tf_op jit(solution)/shard_map/mixer_backward_and_sums/pallas_call | solution.py:1154
  217.1 0.0 copy-start
  217.2 66.7 %gradients_to_owners.1 = (bf16[2,256,1536]{2,1,0:T(8,128)(2,1)}, f32[48,6448]{1,0:T(8,128)}, f32[1,48]{1,0:T(1,128)}, f32[96,1536]{1,0:T(8,128)}, f32[1,96]{1,0:...) custom-call(bf16[1536,2048]{1,0:T(8,128)(2,1)} %get-tuple-element.48.turned_hbm.normed_hbm, ...), custom_call_target="tpu_custom_call" | custom-call | flops 60000002048 | bytes 30000000 | tf_op jit(solution)/shard_map/gradients_to_owners/pallas_call | solution.py:1760
  283.9 0.0 copy-start.1
  283.9 1.3 slice_bitcast_fusion
  285.2 0.0 copy-done
  285.2 1.1 copy.30
  286.4 0.0 copy-done.1
  286.4 0.0 copy-start.5
  286.4 0.0 copy-start.3
  286.4 1.1 copy.31
  287.6 0.0 copy-done.2
  287.6 1.0 copy.32
  288.6 0.0 copy-done.4
  288.6 0.6 copy.33
  289.2 0.0 copy-done.7
  289.2 0.5 copy.34
  289.7 0.0 copy-done.6
  289.7 0.5 copy.35
  290.2 0.0 copy-done.5
  290.2 0.5 copy.36
  290.7 0.8 copy.37
  (5 shorter events, 0.0 us)
Async XLA Ops:
  217.1 68.1 %copy-start = (bf16[2,256,1536]{2,1,0:T(8,128)(2,1)S(1)}, bf16[2,256,1536]{2,1,0:T(8,128)(2,1)}, u32[]{:S(2)}) copy-start(bf16[2,256,1536]{2,1,0:T(8,128)(2,1)} %get-tuple-element.89) | copy-start | bytes 4718596
  283.9 2.5 copy-start.1
  285.2 2.3 copy-start.2
  286.4 2.2 copy-start.4
  286.4 2.8 copy-start.7
  286.4 3.3 %copy-start.6 = (f32[1,48]{1,0:T(1,128)S(1)}, f32[1,48]{1,0:T(1,128)}, u32[]{:S(2)}) copy-start(f32[1,48]{1,0:T(1,128)} %get-tuple-element.72) | copy-start | bytes 580
  286.4 3.8 %copy-start.5 = (f32[1,96]{1,0:T(1,128)S(1)}, f32[1,96]{1,0:T(1,128)}, u32[]{:S(2)}) copy-start(f32[1,96]{1,0:T(1,128)} %get-tuple-element.73) | copy-start | bytes 1156
  286.4 4.3 %copy-start.3 = (f32[96,1536]{1,0:T(8,128)S(1)}, f32[96,1536]{1,0:T(8,128)}, u32[]{:S(2)}) copy-start(f32[96,1536]{1,0:T(8,128)} %get-tuple-element.99) | copy-start | bytes 1769476

commit v5 on v4

--- a/solution.py
+++ b/solution.py
@@ -633,7 +633,7 @@
     chunks = micro * tp
     when = {}
     for n, task in enumerate(tasks):
-        when.setdefault(min(1 + n * 4 // len(tasks), chunks - 1), []).append(plan(*task))
+        when.setdefault(min(2 + n * 4 // len(tasks), chunks - 1), []).append(plan(*task))
     for plans in when.values():
         for steps in plans:
             remember(steps)

time: 292 us -> 292 us (level)
  no operation moved by 1% of the time
where the time goes in v5:
time: 292 us
  Pallas kernels  283 us (97%)
  local copies, waits for them, and re-layouts  7.62 us (3%)
    pallas_call x1, Pallas kernels, head(): pl.pallas_call(functools.partial(head_kernel, dp, heads), in_specs=[vmem]...  101 us
    pallas_call x1, Pallas kernels, middle(): pl.pallas_call(functools.partial(middle_kernel, dp, heads), grid=(micro,...  70.5 us
    pallas_call x1, Pallas kernels, tail(): pl.pallas_call(functools.partial(tail_kernel, dp), in_specs=[hbm] * 9 + [...  66.7 us
    pallas_call x1, Pallas kernels, gating(): pl.pallas_call(functools.partial(gating_kernel, dp), in_specs=[hbm] * 5 +...  44.8 us
    unnamed x24, local copies, waits for them, and re-layouts  6.28 us

profile of v5, /device:TPU:0, one launch (start us, length us, event | category | flops | bytes accessed | tf_op | source)
XLA Modules:
  0.0 291.5 jit_solution(4418967782346562952)
XLA Ops:
  0.6 101.2 %gather_and_mix.1 = (bf16[2,1024,1536]{2,1,0:T(8,128)(2,1)}, bf16[1536,2048]{1,0:T(8,128)(2,1)}, f32[8,256,1152]{2,1,0:T(8,128)}, f32[8,256,768]{2,1,0:T(8,128)}...) custom-call(bf16[48,6448]{1,0:T(8,128)(2,1)} %proj_ref.3, ...), custom_call_target="tpu_custom_call" | custom-call | flops 99999997952 | bytes 50000000 | tf_op jit(solution)/shard_map/gather_and_mix/pallas_call | solution.py:725
  101.9 44.8 %gating_and_gradients.1 = (f32[8,256,768]{2,1,0:T(8,128)}, bf16[8,256,768]{2,1,0:T(8,128)(2,1)}, bf16[8,256,1536]{2,1,0:T(8,128)(2,1)}, bf16[768,1536]{1,0:T(8,128)(2,1)}, bf16[1536,768]{1,0:T(8,128)(2,1)}) custom-call(f32[8,256,768]{2,1,0:T(8,128)} %get-tuple-element.44.ssd_hbm, f32[8,256,768]{2,1,0:T(8,128)} %get-tuple-element.45.gate_hbm, ...), custom_call_target="tpu_custom_call" | custom-call | flops 30000001024 | bytes 50000000 | tf_op jit(solution)/shard_map/gating_and_gradients/pallas_call | solution.py:1379
  146.7 70.5 %mixer_backward_and_sums.1 = (bf16[2048,1152]{1,0:T(8,128)(2,1)}, f32[8,1024]{1,0:T(8,128)}, f32[8,128]{1,0:T(8,128)}, bf16[2,256,1536]{2,1,0:T(8,128)(2,1)}, bf...) custom-call(f32[2048,1152]{1,0:T(8,128)} %bitcast.34, f32[2048,1152]{1,0:T(8,128)} %bitcast.35, ...), custom_call_target="tpu_custom_call" | custom-call | flops 70000001024 | bytes 40000000 | tf_op jit(solution)/shard_map/mixer_backward_and_sums/pallas_call | solution.py:1154
  217.1 0.0 copy-start
  217.2 66.7 %gradients_to_owners.1 = (bf16[2,256,1536]{2,1,0:T(8,128)(2,1)}, f32[48,6448]{1,0:T(8,128)}, f32[1,48]{1,0:T(1,128)}, f32[96,1536]{1,0:T(8,128)}, f32[1,96]{1,0:...) custom-call(bf16[1536,2048]{1,0:T(8,128)(2,1)} %get-tuple-element.48.turned_hbm.normed_hbm, ...), custom_call_target="tpu_custom_call" | custom-call | flops 60000002048 | bytes 30000000 | tf_op jit(solution)/shard_map/gradients_to_owners/pallas_call | solution.py:1760
  283.9 0.0 copy-start.1
  283.9 1.3 slice_bitcast_fusion
  285.2 0.0 copy-done
  285.2 1.1 copy.30
  286.4 0.0 copy-done.1
  286.4 0.0 copy-start.5
  286.4 0.0 copy-start.3
  286.4 1.1 copy.31
  287.6 0.0 copy-done.2
  287.6 1.0 copy.32
  288.6 0.0 copy-done.4
  288.6 0.6 copy.33
  289.2 0.0 copy-done.7
  289.2 0.5 copy.34
  289.7 0.0 copy-done.6
  289.7 0.5 copy.35
  290.2 0.0 copy-done.5
  290.2 0.5 copy.36
  290.7 0.8 copy.37
  (5 shorter events, 0.0 us)
Async XLA Ops:
  217.1 68.1 %copy-start = (bf16[2,256,1536]{2,1,0:T(8,128)(2,1)S(1)}, bf16[2,256,1536]{2,1,0:T(8,128)(2,1)}, u32[]{:S(2)}) copy-start(bf16[2,256,1536]{2,1,0:T(8,128)(2,1)} %get-tuple-element.89) | copy-start | bytes 4718596
  283.9 2.5 copy-start.1
  285.2 2.3 copy-start.2
  286.4 2.2 copy-start.4
  286.4 2.8 copy-start.7
  286.4 3.3 %copy-start.6 = (f32[1,48]{1,0:T(1,128)S(1)}, f32[1,48]{1,0:T(1,128)}, u32[]{:S(2)}) copy-start(f32[1,48]{1,0:T(1,128)} %get-tuple-element.72) | copy-start | bytes 580
  286.4 3.8 %copy-start.5 = (f32[1,96]{1,0:T(1,128)S(1)}, f32[1,96]{1,0:T(1,128)}, u32[]{:S(2)}) copy-start(f32[1,96]{1,0:T(1,128)} %get-tuple-element.73) | copy-start | bytes 1156
  286.4 4.3 %copy-start.3 = (f32[96,1536]{1,0:T(8,128)S(1)}, f32[96,1536]{1,0:T(8,128)}, u32[]{:S(2)}) copy-start(f32[96,1536]{1,0:T(8,128)} %get-tuple-element.99) | copy-start | bytes 1769476
